TPU v7x, 256 devices: a whole 4x4x8 slice. The times are simulated.
256 devices in a mesh: blk: 64 (over y, x_hi, z), grp: 4 (over x_lo, core).
Axes of the slice: x: 4 (x_hi: 2, x_lo: 2; x = x_hi * 2 + x_lo), y: 4, z: 8, core: 2. Of those that a mesh axis runs over, the one named last changes fastest.
Arguments:
- hidden: bfloat16 [524288, 384], P(('blk', 'grp')), may hold values from -6 to 6
- cotangent: bfloat16 [524288, 384], P(('blk', 'grp')), may hold values from -6 to 6
- token_ids: int32 [524288], P(('blk', 'grp')), may hold values from 0 to 32127, as said below
- w_in: bfloat16 [64, 4, 384, 1536], P('blk', 'grp'), may hold values from -6 to 6
- w_out: bfloat16 [1536, 384], replicated, may hold values from -0.15625 to 0.15625
- tracker: bfloat16 [64, 4, 384, 1536], P('blk', 'grp'), may hold values from -6 to 6
- grad_old: bfloat16 [64, 4, 384, 1536], P('blk', 'grp'), may hold values from -6 to 6
- cheb_num: int32 [4], replicated, may hold values from 10 to 16
- cheb_den: int32 [4], replicated, may hold values from 9 to 11
Outputs:
- new_params: bfloat16 [64, 4, 384, 1536], P('blk', 'grp')
- new_tracker: bfloat16 [64, 4, 384, 1536], P('blk', 'grp')
Inputs may be any that keep to these rules, and one draw needn't show every extreme that they name: `token_ids`: each aligned run of 512 rows is one sequence: ids from 1 to 32127 up to its length, 0 after it; every length is 128 or more.
All inputs are finite; a program needn't handle non-finite values.
Results may differ from a plain program's by a relative error of at most 0.013.
Values may be sent and summed in bfloat16 or wider, within the bound.
No kernel may reach another device: no remote copies, remote signals or barrier semaphores. Data moves between devices by JAX's collectives and lax.ppermute only.
A program may use at most 128 MiB of HBM per device.

v0:
```python
import math

import jax
import jax.numpy as jnp
from jax import lax
from jax.sharding import PartitionSpec as P

ROUNDS = 4


epsilon = 1e-06
step_size = 0.25
tanh_scale = math.sqrt(2.0 / math.pi)


def padded(cells, sides, width):
    for axis, dim in sides:
        count = lax.axis_size(axis)
        head = lax.slice_in_dim(cells, 0, width, axis=dim)
        tail = lax.slice_in_dim(cells, cells.shape[dim] - width, cells.shape[dim], axis=dim)
        cells = jnp.concatenate(
            [
                lax.ppermute(tail, axis, [(i, (i + 1) % count) for i in range(count)]),
                cells,
                lax.ppermute(head, axis, [((i + 1) % count, i) for i in range(count)]),
            ],
            axis=dim,
        )
    return cells


def in_blocks(value, dim, devices):
    before, after = (value.shape[:dim], value.shape[dim + 1 :])
    return jnp.moveaxis(value.reshape(*before, devices, -1, *after), dim, 0)


def sent_and_summed(value, axis, dim):
    devices = lax.axis_size(axis)
    tiles = lax.all_to_all(in_blocks(value, dim, devices), axis, 0, 0, tiled=True)
    return jnp.sum(tiles.astype(jnp.float32), axis=0)


def joined_along(tiles, dim):
    shape = list(tiles.shape[1:])
    shape[dim] *= tiles.shape[0]
    return jnp.moveaxis(tiles, 0, dim).reshape(shape)


def copy_for_each(value, axis):
    copies = jnp.broadcast_to(value, (lax.axis_size(axis), *value.shape))
    return lax.all_to_all(copies, axis, split_axis=0, concat_axis=0, tiled=True)


def gathered_copies(value, axis, dim):
    return joined_along(copy_for_each(value, axis), dim)


def gelu_slope(values):
    cubic = values * values * values
    bent_tanh = jnp.tanh(tanh_scale * (values + 0.044715 * cubic))
    return 0.5 * (1.0 + bent_tanh) + 0.5 * values * (1.0 - bent_tanh * bent_tanh) * tanh_scale * (
        1.0 + 3.0 * 0.044715 * values * values
    )


def cycle_mean(beside_all):
    return ((beside_all[0] + beside_all[1] + beside_all[2]) / 3.0)[None]


def local_grad(hidden, cotangent, token_ids, params, w_out):
    widened = hidden.astype(jnp.float32)
    mean_square = jnp.mean(widened * widened, axis=-1, keepdims=True)
    normed = (widened * lax.rsqrt(mean_square + epsilon)).astype(jnp.bfloat16)
    inv_root = params.shape[0] ** (-0.5)
    pre_act = jnp.dot(normed, params, preferred_element_type=jnp.float32) * inv_root
    masked = jnp.where((token_ids != 0)[:, None], cotangent, jnp.zeros_like(cotangent))
    back_flow = lax.dot_general(
        masked, w_out, (((1,), (1,)), ((), ())), preferred_element_type=jnp.float32
    )
    slope_bf = (back_flow * gelu_slope(pre_act)).astype(jnp.bfloat16)
    return (
        lax.dot_general(
            normed, slope_bf, (((0,), (0,)), ((), ())), preferred_element_type=jnp.float32
        )
        * inv_root
    )


def shards(hidden, cotangent, token_ids, w_in, w_out, tracker, grad_old, cheb_num, cheb_den):
    beside_all = padded(w_in, (("blk", 0),), 1).astype(jnp.float32)
    cycle_mixed = cycle_mean(beside_all)
    groups = lax.axis_size("grp")
    part_sum = sent_and_summed(cycle_mixed.astype(jnp.bfloat16), "grp", 3)
    group_avg = gathered_copies((part_sum / groups).astype(jnp.bfloat16), "grp", 3).astype(
        jnp.float32
    )
    new_params = (group_avg - step_size * tracker.astype(jnp.float32)).astype(jnp.bfloat16)
    weights = cheb_num.astype(jnp.float32) / cheb_den.astype(jnp.float32)
    start_iter = tracker.astype(jnp.float32)
    older_iter = start_iter
    current = start_iter
    for turn_idx in range(ROUNDS):
        neighbours = padded(current.astype(jnp.bfloat16), (("blk", 0),), 1).astype(current.dtype)
        next_iter = (
            weights[turn_idx] * cycle_mean(neighbours) + (1.0 - weights[turn_idx]) * older_iter
        )
        older_iter, current = (current, next_iter)
    grad_new = local_grad(hidden, cotangent, token_ids, new_params[0, 0], w_out)[None, None]
    new_tracker = (current + grad_new - grad_old.astype(jnp.float32)).astype(jnp.bfloat16)
    return (new_params, new_tracker)


def solution(mesh):
    placed = (
        P(("blk", "grp"), None),
        P(("blk", "grp"), None),
        P(("blk", "grp")),
        P("blk", "grp", None, None),
        P(),
        P("blk", "grp", None, None),
        P("blk", "grp", None, None),
        P(),
        P(),
    )
    return jax.shard_map(
        shards,
        mesh=mesh,
        in_specs=placed,
        out_specs=(P("blk", "grp", None, None), P("blk", "grp", None, None)),
        check_vma=False,
    )
```

profile of v0, /device:TPU:2, one launch (start us, length us, event | category | flops | bytes accessed | tf_op | source)
XLA Modules:
  0.0 226.4 jit_solution(6230131279533994746)
XLA Ops:
  0.7 1.9 copy.12
  2.5 9.9 %collective-permute-start.1 = (bf16[1,1,384,1536]{2,3,1,0:T(8,128)(2,1)S(1)}, bf16[1,1,384,1536]{2,3,1,0:T(8,128)(2,1)S(1)}, u32[]{:S(2)}, u32[]{:S(2)}) collective-permute-start(bf16[1,1,384,1536]{2,3,1,0:T(8,128)(2,1)S(1)} %copy.12), channel_id=1, source_target_pairs={{4,0},{8,4},{12,8},{16,12},{20,16},{24,20},{28,24},{32,28},{36,32}... | collective-permute-start | bytes 3538952 | tf_op jit(solution)/shard_map/ppermute | solution.py:25
  12.5 7.8 %collective-permute-start.3 = (bf16[1,1,384,1536]{3,2,1,0:T(8,128)(2,1)S(1)}, bf16[1,1,384,1536]{3,2,1,0:T(8,128)(2,1)}, u32[]{:S(2)}, u32[]{:S(2)}) collective-permute-start(bf16[1,1,384,1536]{3,2,1,0:T(8,128)(2,1)S(1)} %copy-done.2), channel_id=1, source_target_pairs={{4,0},{8,4},{12,8},{16,12},{20,16},{24,20},{28,24},{32,28},{36,32}... | collective-permute-start | bytes 3538952 | tf_op jit(solution)/shard_map/ppermute | solution.py:25
  22.2 16.6 %collective-permute-done.1 = bf16[1,1,384,1536]{2,3,1,0:T(8,128)(2,1)S(1)} collective-permute-done((bf16[1,1,384,1536]{2,3,1,0:T(8,128)(2,1)S(1)}, bf16[1,1,384,1536]{2,3,1,0:T(8,128)(2,1)S(1)}, u32[]{:S(2)}, u32[]{:S(2)}) %collective-permute-start.1) | collective-permute-done | bytes 1179680 | tf_op jit(solution)/shard_map/ppermute | solution.py:25
  38.8 8.2 %collective-permute-done = bf16[1,1,384,1536]{2,3,1,0:T(8,128)(2,1)S(1)} collective-permute-done((bf16[1,1,384,1536]{2,3,1,0:T(8,128)(2,1)S(1)}, bf16[1,1,384,1536]{2,3,1,0:T(8,128)(2,1)S(1)}, u32[]{:S(2)}, u32[]{:S(2)}) %collective-permute-start) | collective-permute-done | bytes 1179680 | tf_op jit(solution)/shard_map/ppermute | solution.py:23
  49.5 5.7 %all-to-all-start = ((bf16[4,1,1,384,384]{4,3,2,1,0:T(8,128)(2,1)}), bf16[4,1,1,384,384]{4,3,2,1,0:T(8,128)(2,1)}, u32[]{:S(2)}, u32[]{:S(2)}) async-start(bf16[4,1,1,384,384]{4,3,2,1,0:T(8,128)(2,1)} %copy.15), calls=%async_computation | async-start | bytes 2359296 | tf_op jit(solution)/shard_map/all_to_all | solution.py:39
  55.2 15.9 %collective-permute-done.2 = bf16[1,1,384,1536]{3,2,1,0:T(8,128)(2,1)} collective-permute-done((bf16[1,1,384,1536]{3,2,1,0:T(8,128)(2,1)S(1)}, bf16[1,1,384,1536]{3,2,1,0:T(8,128)(2,1)}, u32[]{:S(2)}, u32[]{:S(2)}) %collective-permute-start.2) | collective-permute-done | bytes 1179680 | tf_op jit(solution)/shard_map/ppermute | solution.py:23
  71.1 2.2 maximum_convert_fusion.1
  73.3 2.4 %fusion.48 = (bf16[1,1,384,1536]{3,2,1,0:T(8,128)(2,1)S(1)}, f32[1,1,384,1536]{3,2,1,0:T(8,128)}) fusion(bf16[1,1,384,1536]{3,2,1,0:T(8,128)(2,1)S(1)} %copy-done.2, f32[]{:T(128)} %bitcast.4, f32[]{:T(128)} %bitcast.3, f32[3,1,384,1536]{3,2,1,0:T(8,128)S(1)} %maximum_convert_fusion.1), kind=kLoop, calls=%fused_computation.67 | loop fusion | flops 4128768 | bytes 11796488 | tf_op jit(solution)/shard_map/convert_element_type | solution.py:103
  76.0 1.8 collective-permute-start.4
  77.7 25.1 %all-to-all-done = bf16[4,1,1,384,384]{4,3,2,1,0:T(8,128)(2,1)} async-done(((bf16[4,1,1,384,384]{4,3,2,1,0:T(8,128)(2,1)}), bf16[4,1,1,384,384]{4,3,2,1,0:T(8,128)(2,1)}, u32[]{:S(2)}, u32[]{:S(2)}) %all-to-all-start) | async-done | bytes 1179680 | tf_op jit(solution)/shard_map/all_to_all | solution.py:39
  105.4 5.7 %all-to-all-start.1 = ((bf16[4,1,1,384,384]{4,3,2,1,0:T(8,128)(2,1)}), bf16[4,1,1,384,384]{4,3,2,1,0:T(8,128)(2,1)}, u32[]{:S(2)}, u32[]{:S(2)}) async-start(bf16[4,1,1,384,384]{4,3,2,1,0:T(8,128)(2,1)} %broadcast_in_dim.11), calls=%async_computation.1 | async-start | bytes 2359296 | tf_op jit(solution)/shard_map/all_to_all | solution.py:51
  112.5 5.0 %maximum_convert_fusion.2 = f32[3,1,384,1536]{3,2,1,0:T(8,128)} fusion(bf16[1,1,384,1536]{3,2,1,0:T(8,128)(2,1)} %collective-permute-done.5, bf16[1,1,384,1536]{3,2,1,0:T(8,128)(2,1)S(1)} %get-tuple-element.4, bf16[1,1,384,1536]{3,2,1,0:T(8,128)(2,1)} %collective-permute-done.4), kind=kLoop, calls=%fused_computation.10 | loop fusion | flops 5308416 | bytes 10616832 | tf_op jit(solution)/shard_map/convert_element_type | solution.py:103
  117.5 8.0 %all-to-all-done.1 = bf16[4,1,1,384,384]{4,3,2,1,0:T(8,128)(2,1)} async-done(((bf16[4,1,1,384,384]{4,3,2,1,0:T(8,128)(2,1)}), bf16[4,1,1,384,384]{4,3,2,1,0:T(8,128)(2,1)}, u32[]{:S(2)}, u32[]{:S(2)}) %all-to-all-start.1) | async-done | bytes 1179680 | tf_op jit(solution)/shard_map/all_to_all | solution.py:51
  128.8 2.7 %fusion.46 = (bf16[1,1,384,1536]{3,2,1,0:T(8,128)(2,1)S(1)}, f32[1,1,384,1536]{3,2,1,0:T(8,128)}, bf16[1,1,384,1536]{3,2,1,0:T(8,128)(2,1)S(1)}) fusion(bf16[1,1,384,1536]{3,2,1,0:T(8,128)(2,1)S(1)} %copy-done.2, f32[]{:T(128)} %bitcast.6, f32[]{:T(128)} %bitcast.5, f32[3,1,384,1536]{3,2,1,0:T(8,128)S(1)} %copy-done.1, f32[1,1,384,1536]{3,2,1,0:T(8,128)S(1)} %bitcast.23), kind=kLoop, calls=%fused_computation.66 | loop fusion | flops 5898240 | bytes 15335432 | tf_op jit(solution)/shard_map/convert_element_type | solution.py:103
  131.5 2.7 %collective-permute-start.7 = (bf16[1,1,384,1536]{3,2,1,0:T(8,128)(2,1)S(1)}, bf16[1,1,384,1536]{3,2,1,0:T(8,128)(2,1)S(1)}, u32[]{:S(2)}, u32[]{:S(2)}) collective-permute-start(bf16[1,1,384,1536]{3,2,1,0:T(8,128)(2,1)S(1)} %get-tuple-element.2), channel_id=1, source_target_pairs={{4,0},{8,4},{12,8},{16,12},{20,16},{24,20},{28,24},{32,28},{36,32}... | collective-permute-start | bytes 3538952 | tf_op jit(solution)/shard_map/ppermute | solution.py:25
  136.7 22.9 %collective-permute-done.7 = bf16[1,1,384,1536]{3,2,1,0:T(8,128)(2,1)S(1)} collective-permute-done((bf16[1,1,384,1536]{3,2,1,0:T(8,128)(2,1)S(1)}, bf16[1,1,384,1536]{3,2,1,0:T(8,128)(2,1)S(1)}, u32[]{:S(2)}, u32[]{:S(2)}) %collective-permute-start.7) | collective-permute-done | bytes 1179680 | tf_op jit(solution)/shard_map/ppermute | solution.py:25
  159.6 7.9 %collective-permute-done.6 = bf16[1,1,384,1536]{3,2,1,0:T(8,128)(2,1)S(1)} collective-permute-done((bf16[1,1,384,1536]{3,2,1,0:T(8,128)(2,1)S(1)}, bf16[1,1,384,1536]{3,2,1,0:T(8,128)(2,1)S(1)}, u32[]{:S(2)}, u32[]{:S(2)}) %collective-permute-start.6) | collective-permute-done | bytes 1179680 | tf_op jit(solution)/shard_map/ppermute | solution.py:23
  169.6 1.7 collective-permute-start.8
  171.7 6.4 %fusion.31 = f32[2048,1536]{1,0:T(8,128)} fusion(bf16[1,1,384,1536]{3,2,1,0:T(8,128)(2,1)S(1)} %get-tuple-element.6, bf16[2048,384]{1,0:T(8,128)(2,1)S(1)} %copy-done.4, f32[2048]{0:T(1024)S(1)} %add_rsqrt_fusion), kind=kOutput, calls=%fused_computation.51 | convolution fusion | flops 2418278400 | bytes 15343616 | tf_op jit(solution)/shard_map/dot_general | solution.py:75
  178.2 17.8 %collective-permute-done.9 = bf16[1,1,384,1536]{3,2,1,0:T(8,128)(2,1)S(1)} collective-permute-done((bf16[1,1,384,1536]{3,2,1,0:T(8,128)(2,1)S(1)}, bf16[1,1,384,1536]{3,2,1,0:T(8,128)(2,1)S(1)}, u32[]{:S(2)}, u32[]{:S(2)}) %collective-permute-start.9) | collective-permute-done | bytes 1179680 | tf_op jit(solution)/shard_map/ppermute | solution.py:25
  195.9 6.0 %collective-permute-done.8 = bf16[1,1,384,1536]{3,2,1,0:T(8,128)(2,1)S(1)} collective-permute-done((bf16[1,1,384,1536]{3,2,1,0:T(8,128)(2,1)S(1)}, bf16[1,1,384,1536]{3,2,1,0:T(8,128)(2,1)S(1)}, u32[]{:S(2)}, u32[]{:S(2)}) %collective-permute-start.8) | collective-permute-done | bytes 1179680 | tf_op jit(solution)/shard_map/ppermute | solution.py:23
  201.9 3.4 %maximum_convert_fusion.4 = f32[3,1,384,1536]{3,2,1,0:T(8,128)} fusion(bf16[1,1,384,1536]{3,2,1,0:T(8,128)(2,1)S(1)} %collective-permute-done.9, bf16[1,1,384,1536]{3,2,1,0:T(8,128)(2,1)S(1)} %fusion.20, bf16[1,1,384,1536]{3,2,1,0:T(8,128)(2,1)S(1)} %collective-permute-done.8), kind=kLoop, calls=%fused_computation.12 | loop fusion | flops 5308416 | bytes 10616832 | tf_op jit(solution)/shard_map/convert_element_type | solution.py:103
  205.3 21.1 %fusion.17 = bf16[1,1,384,1536]{3,2,1,0:T(8,128)(2,1)} fusion(f32[3,1,384,1536]{3,2,1,0:T(8,128)} %maximum_convert_fusion.4, bf16[1,1,384,1536]{3,2,1,0:T(8,128)(2,1)} %param.15, f32[1,1,384,1536]{3,2,1,0:T(8,128)} %get-tuple-element.3, f32[2048,1536]{1,0:T(8,128)} %fusion.31, bf16[1536,384]{1,0:T(8,128)(2,1)S(1)} %copy-done, bf16[2048,384]{1,0:T(8,128)(2,1)} %param.10, ...), kind=kOutput, calls=%fused_computation.30 | convolution fusion | flops 4903796736 | bytes 28715016 | tf_op jit(solution)/shard_map/dot_general | solution.py:82
  (41 shorter events, 11.9 us)
Async XLA Ops:
  0.6 204.7 %copy-start = (bf16[1536,384]{1,0:T(8,128)(2,1)S(1)}, bf16[1536,384]{1,0:T(8,128)(2,1)}, u32[]{:S(2)}) copy-start(bf16[1536,384]{1,0:T(8,128)(2,1)} %param.13) | copy-start | bytes 3538948
  0.6 11.8 %copy-start.2 = (bf16[1,1,384,1536]{3,2,1,0:T(8,128)(2,1)S(1)}, bf16[1,1,384,1536]{3,2,1,0:T(8,128)(2,1)}, u32[]{:S(2)}) copy-start(bf16[1,1,384,1536]{3,2,1,0:T(8,128)(2,1)} %param.14) | copy-start | bytes 3538948
  0.7 19.6 %copy-start.7 = (s32[4]{0:T(128)S(1)}, s32[4]{0:T(128)}, u32[]{:S(2)}) copy-start(s32[4]{0:T(128)} %param.17) | copy-start | bytes 52
  0.7 19.6 %copy-start.8 = (s32[4]{0:T(128)S(1)}, s32[4]{0:T(128)}, u32[]{:S(2)}) copy-start(s32[4]{0:T(128)} %param.16) | copy-start | bytes 52
  2.5 36.3 %collective-permute-start.1 = (bf16[1,1,384,1536]{2,3,1,0:T(8,128)(2,1)S(1)}, bf16[1,1,384,1536]{2,3,1,0:T(8,128)(2,1)S(1)}, u32[]{:S(2)}, u32[]{:S(2)}) collective-permute-start(bf16[1,1,384,1536]{2,3,1,0:T(8,128)(2,1)S(1)} %copy.12), channel_id=1, source_target_pairs={{4,0},{8,4},{12,8},{16,12},{20,16},{24,20},{28,24},{32,28},{36,32}... | collective-permute-start | bytes 3538952 | tf_op jit(solution)/shard_map/ppermute | solution.py:25
  12.5 34.6 %collective-permute-start = (bf16[1,1,384,1536]{2,3,1,0:T(8,128)(2,1)S(1)}, bf16[1,1,384,1536]{2,3,1,0:T(8,128)(2,1)S(1)}, u32[]{:S(2)}, u32[]{:S(2)}) collective-permute-start(bf16[1,1,384,1536]{2,3,1,0:T(8,128)(2,1)S(1)} %copy.12), channel_id=1, source_target_pairs={{0,4},{4,8},{8,12},{12,16},{16,20},{20,24},{24,28},{28,32},{32,36}... | collective-permute-start | bytes 3538952 | tf_op jit(solution)/shard_map/ppermute | solution.py:23
  12.5 58.6 %collective-permute-start.2 = (bf16[1,1,384,1536]{3,2,1,0:T(8,128)(2,1)S(1)}, bf16[1,1,384,1536]{3,2,1,0:T(8,128)(2,1)}, u32[]{:S(2)}, u32[]{:S(2)}) collective-permute-start(bf16[1,1,384,1536]{3,2,1,0:T(8,128)(2,1)S(1)} %copy-done.2), channel_id=1, source_target_pairs={{0,4},{4,8},{8,12},{12,16},{16,20},{20,24},{24,28},{28,32},{32,36}... | collective-permute-start | bytes 3538952 | tf_op jit(solution)/shard_map/ppermute | solution.py:23
  12.5 58.6 %collective-permute-start.3 = (bf16[1,1,384,1536]{3,2,1,0:T(8,128)(2,1)S(1)}, bf16[1,1,384,1536]{3,2,1,0:T(8,128)(2,1)}, u32[]{:S(2)}, u32[]{:S(2)}) collective-permute-start(bf16[1,1,384,1536]{3,2,1,0:T(8,128)(2,1)S(1)} %copy-done.2), channel_id=1, source_target_pairs={{4,0},{8,4},{12,8},{16,12},{20,16},{24,20},{28,24},{32,28},{36,32}... | collective-permute-start | bytes 3538952 | tf_op jit(solution)/shard_map/ppermute | solution.py:25
  49.5 53.3 %all-to-all-start = ((bf16[4,1,1,384,384]{4,3,2,1,0:T(8,128)(2,1)}), bf16[4,1,1,384,384]{4,3,2,1,0:T(8,128)(2,1)}, u32[]{:S(2)}, u32[]{:S(2)}) async-start(bf16[4,1,1,384,384]{4,3,2,1,0:T(8,128)(2,1)} %copy.15), calls=%async_computation | async-start | bytes 2359296 | tf_op jit(solution)/shard_map/all_to_all | solution.py:39
  75.7 36.8 %collective-permute-start.5 = (bf16[1,1,384,1536]{3,2,1,0:T(8,128)(2,1)S(1)}, bf16[1,1,384,1536]{3,2,1,0:T(8,128)(2,1)}, u32[]{:S(2)}, u32[]{:S(2)}) collective-permute-start(bf16[1,1,384,1536]{3,2,1,0:T(8,128)(2,1)S(1)} %get-tuple-element.4), channel_id=1, source_target_pairs={{4,0},{8,4},{12,8},{16,12},{20,16},{24,20},{28,24},{32,28},{36,32}... | collective-permute-start | bytes 3538952 | tf_op jit(solution)/shard_map/ppermute | solution.py:25
  76.0 36.5 %collective-permute-start.4 = (bf16[1,1,384,1536]{3,2,1,0:T(8,128)(2,1)S(1)}, bf16[1,1,384,1536]{3,2,1,0:T(8,128)(2,1)}, u32[]{:S(2)}, u32[]{:S(2)}) collective-permute-start(bf16[1,1,384,1536]{3,2,1,0:T(8,128)(2,1)S(1)} %get-tuple-element.4), channel_id=1, source_target_pairs={{0,4},{4,8},{8,12},{12,16},{16,20},{20,24},{24,28},{28,32},{32,36}... | collective-permute-start | bytes 3538952 | tf_op jit(solution)/shard_map/ppermute | solution.py:23
  105.4 20.0 %all-to-all-start.1 = ((bf16[4,1,1,384,384]{4,3,2,1,0:T(8,128)(2,1)}), bf16[4,1,1,384,384]{4,3,2,1,0:T(8,128)(2,1)}, u32[]{:S(2)}, u32[]{:S(2)}) async-start(bf16[4,1,1,384,384]{4,3,2,1,0:T(8,128)(2,1)} %broadcast_in_dim.11), calls=%async_computation.1 | async-start | bytes 2359296 | tf_op jit(solution)/shard_map/all_to_all | solution.py:51
  125.5 3.4 %copy-start.1 = (f32[3,1,384,1536]{3,2,1,0:T(8,128)S(1)}, f32[3,1,384,1536]{3,2,1,0:T(8,128)}, u32[]{:S(2)}) copy-start(f32[3,1,384,1536]{3,2,1,0:T(8,128)} %maximum_convert_fusion.2) | copy-start | bytes 21233668
  131.5 40.2 %copy-start.5 = (bf16[1,1,384,1536]{3,2,1,0:T(8,128)(2,1)}, bf16[1,1,384,1536]{3,2,1,0:T(8,128)(2,1)S(1)}, u32[]{:S(2)}) copy-start(bf16[1,1,384,1536]{3,2,1,0:T(8,128)(2,1)S(1)} %get-tuple-element.6) | copy-start | bytes 3538948
  131.5 28.0 %collective-permute-start.7 = (bf16[1,1,384,1536]{3,2,1,0:T(8,128)(2,1)S(1)}, bf16[1,1,384,1536]{3,2,1,0:T(8,128)(2,1)S(1)}, u32[]{:S(2)}, u32[]{:S(2)}) collective-permute-start(bf16[1,1,384,1536]{3,2,1,0:T(8,128)(2,1)S(1)} %get-tuple-element.2), channel_id=1, source_target_pairs={{4,0},{8,4},{12,8},{16,12},{20,16},{24,20},{28,24},{32,28},{36,32}... | collective-permute-start | bytes 3538952 | tf_op jit(solution)/shard_map/ppermute | solution.py:25
  134.3 33.2 %collective-permute-start.6 = (bf16[1,1,384,1536]{3,2,1,0:T(8,128)(2,1)S(1)}, bf16[1,1,384,1536]{3,2,1,0:T(8,128)(2,1)S(1)}, u32[]{:S(2)}, u32[]{:S(2)}) collective-permute-start(bf16[1,1,384,1536]{3,2,1,0:T(8,128)(2,1)S(1)} %get-tuple-element.2), channel_id=1, source_target_pairs={{0,4},{4,8},{8,12},{12,16},{16,20},{20,24},{24,28},{28,32},{32,36}... | collective-permute-start | bytes 3538952 | tf_op jit(solution)/shard_map/ppermute | solution.py:23
  136.7 31.4 %copy-start.3 = (f32[1,1,384,1536]{3,2,1,0:T(8,128)S(1)}, f32[1,1,384,1536]{3,2,1,0:T(8,128)}, u32[]{:S(2)}) copy-start(f32[1,1,384,1536]{3,2,1,0:T(8,128)} %get-tuple-element.5) | copy-start | bytes 7077892
  168.0 3.3 %copy-start.4 = (bf16[2048,384]{1,0:T(8,128)(2,1)S(1)}, bf16[2048,384]{1,0:T(8,128)(2,1)}, u32[]{:S(2)}) copy-start(bf16[2048,384]{1,0:T(8,128)(2,1)} %param.9) | copy-start | bytes 4718596
  168.1 3.6 %copy-start.6 = (s32[2048]{0:T(1024)S(1)}, s32[2048]{0:T(1024)}, u32[]{:S(2)}) copy-start(s32[2048]{0:T(1024)} %param.11) | copy-start | bytes 24580
  169.2 26.7 %collective-permute-start.9 = (bf16[1,1,384,1536]{3,2,1,0:T(8,128)(2,1)S(1)}, bf16[1,1,384,1536]{3,2,1,0:T(8,128)(2,1)S(1)}, u32[]{:S(2)}, u32[]{:S(2)}) collective-permute-start(bf16[1,1,384,1536]{3,2,1,0:T(8,128)(2,1)S(1)} %fusion.20), channel_id=1, source_target_pairs={{4,0},{8,4},{12,8},{16,12},{20,16},{24,20},{28,24},{32,28},{36,32}... | collective-permute-start | bytes 3538952 | tf_op jit(solution)/shard_map/ppermute | solution.py:25
  169.6 32.4 %collective-permute-start.8 = (bf16[1,1,384,1536]{3,2,1,0:T(8,128)(2,1)S(1)}, bf16[1,1,384,1536]{3,2,1,0:T(8,128)(2,1)S(1)}, u32[]{:S(2)}, u32[]{:S(2)}) collective-permute-start(bf16[1,1,384,1536]{3,2,1,0:T(8,128)(2,1)S(1)} %fusion.20), channel_id=1, source_target_pairs={{0,4},{4,8},{8,12},{12,16},{16,20},{20,24},{24,28},{28,32},{32,36}... | collective-permute-start | bytes 3538952 | tf_op jit(solution)/shard_map/ppermute | solution.py:23
where the time goes:
time: 227 us; the launch traced here: 226 us
  waiting for transfers between devices  128 us (56%)
  starting transfers between devices  35.9 us (16%)
  matrix products  27.5 us (12%)
  other arithmetic  21.9 us (10%)
  local copies, waits for them, and re-layouts  6.89 us (3%)
  between operations  5.81 us (3%)
    ppermute x5, waiting for transfers between devices, padded(): lax.ppermute(head, axis, [((i + 1) % count, i) for i in range(count)])  57.3 us
    ppermute x5, waiting for transfers between devices, padded(): lax.ppermute(tail, axis, [(i, (i + 1) % count) for i in range(count)])  38.1 us
    all_to_all x1, waiting for transfers between devices, sent_and_summed(): lax.all_to_all(in_blocks(value, dim, devices), axis, 0, 0, tiled=True)  25.1 us
    dot_general x1, matrix products, local_grad(): lax.dot_general(normed, slope_bf, (((0,), (0,)), ((), ())), preferred_ele...  21.1 us
    ppermute x5, starting transfers between devices, padded(): lax.ppermute(head, axis, [((i + 1) % count, i) for i in range(count)])  21.1 us
    convert_element_type x4, other arithmetic, shards(): padded(current.astype(jnp.bfloat16), (('blk', 0),), 1).astype(current.dtype)  11.1 us
    all_to_all x1, waiting for transfers between devices, copy_for_each(): return lax.all_to_all(copies, axis, split_axis=0, concat_axis=0, tiled=True)  7.95 us
    dot_general x1, matrix products, local_grad(): jnp.dot(normed, params, preferred_element_type=jnp.float32) * inv_root  6.41 us
  transfers between devices with their start and end apart: 12, of which 9 were waited for; matrix products, arithmetic and copies ran while one was open for 10% of the time, Pallas kernels for 0%

commit v1 on v0

v1 whole, which is shorter than its diff:
```python
import math

import jax
import jax.numpy as jnp
from jax import lax
from jax.experimental import pallas as pl
from jax.experimental.pallas import tpu as pltpu
from jax.sharding import PartitionSpec as P


ROUNDS = 4

epsilon = 1e-06
step_size = 0.25
tanh_scale = math.sqrt(2.0 / math.pi)

f32 = jnp.float32
bf16 = jnp.bfloat16


def slope_of(scaled, back_flow, inv_root):
    lead, bend = tanh_scale * inv_root, tanh_scale * 0.044715 * inv_root**3
    square = scaled * scaled
    half = 0.5 * jnp.tanh(scaled * (lead + bend * square)) + 0.5
    inner = scaled * (2.0 * lead + 6.0 * bend * square)
    return back_flow * (half + half * (1.0 - half) * inner)


def grad_body(
    place_ref,
    normed_ref,
    turned_ref,
    masked_ref,
    first_ref,
    second_ref,
    third_ref,
    fourth_ref,
    tracker_ref,
    w_out_ref,
    old_ref,
    params_ref,
    out_ref,
    mixed_ref,
    slope_ref,
):
    tokens, width = normed_ref.shape
    inv_root = width ** (-0.5)
    quarter = width // 4
    for k, part_ref in enumerate((first_ref, second_ref, third_ref, fourth_ref)):
        at = pl.multiple_of(place_ref[k] * quarter, quarter)
        mixed_ref[pl.ds(at, quarter)] = part_ref[...]
    params_ref[...] = (
        mixed_ref[...].astype(f32) - step_size * tracker_ref[...].astype(f32)
    ).astype(bf16)
    step = 256
    held = None
    for at in range(0, tokens + step, step):
        ready = held
        if at < tokens:
            rows = pl.ds(at, step)
            scaled = jnp.dot(normed_ref[rows], params_ref[...], preferred_element_type=f32)
            back_flow = lax.dot_general(
                masked_ref[rows],
                w_out_ref[...],
                (((1,), (1,)), ((), ())),
                preferred_element_type=f32,
            )
            held = (rows, scaled, back_flow)
        if ready is not None:
            rows, scaled, back_flow = ready
            slope_ref[rows] = slope_of(scaled, back_flow, inv_root).astype(bf16)
    grad = jnp.dot(turned_ref[...], slope_ref[...], preferred_element_type=f32)
    out_ref[...] = grad * inv_root - old_ref[...].astype(f32)


def grad_change(place, normed, turned, masked, parts, tracker, w_out, grad_old):
    tokens, width = normed.shape
    hidden = tracker.shape[1]
    block = 256
    whole = pl.BlockSpec(memory_space=pltpu.VMEM)
    column = pl.BlockSpec((width, block), lambda j: (0, j))
    piece = pl.BlockSpec((width // 4, block), lambda j: (0, j))
    return pl.pallas_call(
        grad_body,
        grid=(hidden // block,),
        out_shape=(
            jax.ShapeDtypeStruct((width, hidden), bf16),
            jax.ShapeDtypeStruct((width, hidden), f32),
        ),
        in_specs=[
            pl.BlockSpec(memory_space=pltpu.SMEM),
            whole,
            whole,
            whole,
            piece,
            piece,
            piece,
            piece,
            column,
            pl.BlockSpec((block, width), lambda j: (j, 0)),
            column,
        ],
        out_specs=(column, column),
        scratch_shapes=[pltpu.VMEM((width, block), bf16), pltpu.VMEM((tokens, block), bf16)],
        cost_estimate=pl.CostEstimate(
            flops=6 * tokens * width * hidden,
            bytes_accessed=14 * width * hidden,
            transcendentals=tokens * hidden,
        ),
        name="grad_change",
    )(place, normed, turned, masked, *parts, tracker, w_out, grad_old)


def normed_of(hidden):
    widened = hidden.astype(f32)
    mean_square = jnp.mean(widened * widened, axis=-1, keepdims=True)
    return (widened * lax.rsqrt(mean_square + epsilon)).astype(bf16)


def shift(value, axis, step):
    count = lax.axis_size(axis)
    return lax.ppermute(value, axis, [(i, (i + step) % count) for i in range(count)])


def swap(value, bit):
    count = lax.axis_size("grp")
    return lax.ppermute(value, "grp", [(i, i ^ bit) for i in range(count)])


def stencil_taps(num_ref, den_ref):
    def wide(value):
        return jnp.full((8, 128), value, f32)

    weights = [
        wide(num_ref[t].astype(f32)) / wide(den_ref[t].astype(f32)) for t in range(ROUNDS)
    ]
    zero = wide(0.0)
    older = [wide(1.0)] + [zero] * ROUNDS
    current = older
    for t in range(ROUNDS):
        mean = []
        for d in range(ROUNDS + 1):
            left = current[d - 1] if d > 0 else current[1]
            right = current[d + 1] if d < ROUNDS else zero
            mean.append((left + current[d] + right) / 3.0)
        following = [weights[t] * m + (1.0 - weights[t]) * o for m, o in zip(mean, older)]
        older, current = current, following
    return current


def stencil_body(num_ref, den_ref, cells_ref, out_ref, wide_ref):
    workers, rows, _ = cells_ref.shape
    wide_ref[pl.ds(ROUNDS, workers)] = cells_ref[...].astype(f32)
    wide_ref[pl.ds(0, ROUNDS)] = cells_ref[pl.ds(workers - ROUNDS, ROUNDS)].astype(f32)
    wide_ref[pl.ds(ROUNDS + workers, ROUNDS)] = cells_ref[pl.ds(0, ROUNDS)].astype(f32)
    taps = [jnp.tile(t, (rows // 8, 1)) for t in stencil_taps(num_ref, den_ref)]

    def one(b, carry):
        total = taps[0] * wide_ref[b + ROUNDS]
        for d in range(1, ROUNDS + 1):
            total = total + taps[d] * (wide_ref[b + ROUNDS - d] + wide_ref[b + ROUNDS + d])
        out_ref[b] = total.astype(bf16)
        return carry

    lax.fori_loop(0, workers, one, 0, unroll=4)


def stencil(cells, cheb_num, cheb_den):
    workers, rows, lanes = cells.shape
    block = 24 if rows % 24 == 0 else rows
    spec = pl.BlockSpec((workers, block, lanes), lambda i: (0, i, 0))
    return pl.pallas_call(
        stencil_body,
        grid=(rows // block,),
        out_shape=jax.ShapeDtypeStruct(cells.shape, bf16),
        in_specs=[
            pl.BlockSpec(memory_space=pltpu.SMEM),
            pl.BlockSpec(memory_space=pltpu.SMEM),
            spec,
        ],
        out_specs=spec,
        scratch_shapes=[pltpu.VMEM((workers + 2 * ROUNDS, block, lanes), f32)],
        cost_estimate=pl.CostEstimate(
            flops=14 * cells.size, bytes_accessed=4 * cells.size, transcendentals=0
        ),
        name="stencil",
    )(cheb_num, cheb_den, cells)


def to_tiles(value, workers):
    rows, cols = value.shape
    tiles = value.reshape(rows // 8, 8, cols // 128, 128).transpose(0, 2, 1, 3)
    return tiles.reshape(workers, rows * cols // (128 * workers), 128)


def from_tiles(tiles, rows, cols):
    value = tiles.reshape(rows // 8, cols // 128, 8, 128).transpose(0, 2, 1, 3)
    return value.reshape(rows, cols)


def consensus_of(tracker, cheb_num, cheb_den):
    workers = lax.axis_size("blk")
    cells = to_tiles(tracker, workers)
    cells = lax.all_to_all(cells, "blk", 0, 0, tiled=True)
    cells = stencil(cells, cheb_num, cheb_den)
    cells = lax.all_to_all(cells, "blk", 0, 0, tiled=True)
    return from_tiles(cells, *tracker.shape)


def mixed_of(w_in):
    rows = w_in.shape[0]
    half, quarter = rows // 2, rows // 4
    member = lax.axis_index("grp")
    core, chip = member % 2, member // 2
    other = lax.dynamic_slice_in_dim(w_in, (1 - core) * half, half, 0)
    mine = lax.dynamic_slice_in_dim(w_in, core * half, half, 0)
    pair = mine.astype(f32) + swap(other, 1).astype(f32)
    other = lax.dynamic_slice_in_dim(pair, (1 - chip) * quarter, quarter, 0).astype(bf16)
    mine = lax.dynamic_slice_in_dim(pair, chip * quarter, quarter, 0)
    total = mine + swap(other, 2).astype(f32)
    sent = total.astype(bf16)
    below, above = shift(sent, "blk", 1), shift(sent, "blk", -1)
    mean = ((below.astype(f32) + total + above.astype(f32)) / 3.0 / 4.0).astype(bf16)
    far = swap(mean, 2)
    near = swap(mean, 1)
    last = swap(far, 1)
    place = jnp.stack(
        [
            core * 2 + chip,
            core * 2 + 1 - chip,
            (1 - core) * 2 + chip,
            (1 - core) * 2 + 1 - chip,
        ]
    ).astype(jnp.int32)
    return place, (mean, far, near, last)


def shards(hidden, cotangent, token_ids, w_in, w_out, tracker, grad_old, cheb_num, cheb_den):
    consensus = consensus_of(tracker[0, 0], cheb_num, cheb_den)
    place, parts = mixed_of(w_in[0, 0])
    normed = normed_of(hidden)
    masked = jnp.where((token_ids != 0)[:, None], cotangent, jnp.zeros_like(cotangent))
    normed, turned, masked = lax.optimization_barrier((normed, normed.T, masked))
    new_params, change = grad_change(
        place, normed, turned, masked, parts, tracker[0, 0], w_out, grad_old[0, 0]
    )
    new_tracker = (consensus.astype(f32) + change).astype(bf16)
    return (new_params[None, None], new_tracker[None, None])


def solution(mesh):
    placed = (
        P(("blk", "grp"), None),
        P(("blk", "grp"), None),
        P(("blk", "grp")),
        P("blk", "grp", None, None),
        P(),
        P("blk", "grp", None, None),
        P("blk", "grp", None, None),
        P(),
        P(),
    )
    return jax.shard_map(
        shards,
        mesh=mesh,
        in_specs=placed,
        out_specs=(P("blk", "grp", None, None), P("blk", "grp", None, None)),
        check_vma=False,
    )
```

time: 227 us -> 101 us (0.44)
  waiting for transfers between devices: 128 us -> 31.4 us
  matrix products: 27.5 us -> 0 us
  Pallas kernels: 0 us -> 19.4 us
  other arithmetic: 21.9 us -> 11 us
  starting transfers between devices: 35.9 us -> 30.3 us
  between operations: 5.81 us -> 0.87 us
    ppermute x10 -> x7, waiting for transfers between devices: 95.3 us -> 22.5 us  [the longest x5 22.4 us: swap(): return lax.ppermute(value, 'grp', [(i, i ^ bit) for i in range(count)])]
    dot_general x2 -> x0, matrix products: 27.5 us -> none  [the longest x1 21.1 us: local_grad(): lax.dot_general(normed, slope_bf, (((0,), (0,)), ((), ())), preferred_ele...]
    all_to_all x2, waiting for transfers between devices: 33 us -> 8.97 us  [consensus_of(): cells = lax.all_to_all(cells, 'blk', 0, 0, tiled=True)]
    pallas_call x0 -> x2, Pallas kernels: none -> 19.4 us  [the longest x1 15.5 us: grad_change(): pl.pallas_call(grad_body, grid=(hidden // block,), out_shape=(jax.ShapeDt...]
    convert_element_type x10 -> x3, other arithmetic: 18.4 us -> 2.34 us  [the longest x1 1.2 us: mixed_of(): ((below.astype(f32) + total + above.astype(f32)) / 3.0 / 4.0).astype(bf16)]
    ppermute x10 -> x7, starting transfers between devices: 24.6 us -> 10.9 us  [the longest x2 7.75 us: shift(): lax.ppermute(value, axis, [(i, (i + step) % count) for i in range(count)])]
    all_to_all x2, starting transfers between devices: 11.4 us -> 19.4 us  [consensus_of(): cells = lax.all_to_all(cells, 'blk', 0, 0, tiled=True)]
    broadcast_in_dim x0 -> x1, other arithmetic: none -> 3.32 us  [shards(): return (new_params[None, None], new_tracker[None, None])]
  transfers between devices with their start and end apart: 12 -> 9, of which waited for: 9 -> 3; matrix products, arithmetic and copies ran while one was open for 10% -> 10% of each run, Pallas kernels for 0% -> 20%
where the time goes in v1:
time: 101 us; the launch traced here: 99 us
  waiting for transfers between devices  31.4 us (31%)
  starting transfers between devices  30.3 us (30%)
  Pallas kernels  19.4 us (19%)
  other arithmetic  11 us (11%)
  local copies, waits for them, and re-layouts  5.98 us (6%)
    ppermute x5, waiting for transfers between devices, swap(): return lax.ppermute(value, 'grp', [(i, i ^ bit) for i in range(count)])  22.4 us
    all_to_all x2, starting transfers between devices, consensus_of(): cells = lax.all_to_all(cells, 'blk', 0, 0, tiled=True)  19.4 us
    pallas_call x1, Pallas kernels, grad_change(): pl.pallas_call(grad_body, grid=(hidden // block,), out_shape=(jax.ShapeDt...  15.5 us
    all_to_all x2, waiting for transfers between devices, consensus_of(): cells = lax.all_to_all(cells, 'blk', 0, 0, tiled=True)  8.97 us
    ppermute x2, starting transfers between devices, shift(): lax.ppermute(value, axis, [(i, (i + step) % count) for i in range(count)])  7.75 us
    pallas_call x1, Pallas kernels, stencil(): pl.pallas_call(stencil_body, grid=(rows // block,), out_shape=jax.ShapeDt...  3.99 us
    broadcast_in_dim x1, other arithmetic, shards(): return (new_params[None, None], new_tracker[None, None])  3.32 us
    ppermute x5, starting transfers between devices, swap(): return lax.ppermute(value, 'grp', [(i, i ^ bit) for i in range(count)])  3.14 us
  transfers between devices with their start and end apart: 9, of which 3 were waited for; matrix products, arithmetic and copies ran while one was open for 10% of the time, Pallas kernels for 20%

profile of v1, /device:TPU:2, one launch (start us, length us, event | category | flops | bytes accessed | tf_op | source)
XLA Modules:
  0.0 99.0 jit_solution(2580802531820466503)
XLA Ops:
  0.7 2.0 %dynamic-slice_bitcast_fusion = bf16[192,1536]{1,0:T(8,128)(2,1)} fusion(bf16[1,1,384,1536]{3,2,1,0:T(8,128)(2,1)} %param.12, s32[]{:T(128)S(6)} %select_n.31), kind=kLoop, calls=%fused_computation.12 | loop fusion | bytes 1179652 | tf_op jit(solution)/shard_map/dynamic_slice | solution.py:215
  2.7 13.9 %all-to-all-start = ((bf16[64,72,128]{2,1,0:T(8,128)(2,1)}), bf16[64,72,128]{2,1,0:T(8,128)(2,1)}, u32[]{:S(2)}, u32[]{:S(2)}) async-start(bf16[64,72,128]{2,1,0:T(8,128)(2,1)} %bitcast.31), calls=%async_computation | async-start | bytes 2359296 | tf_op jit(solution)/shard_map/all_to_all | solution.py:204
  16.6 0.8 copy.11
  17.4 1.4 %convert_add_fusion = f32[192,1536]{1,0:T(8,128)S(1)} fusion(bf16[192,1536]{1,0:T(8,128)(2,1)} %collective-permute-done, bf16[1,1,384,1536]{3,2,1,0:T(8,128)(2,1)} %param.12, s32[]{:T(128)S(6)} %select_n.30), kind=kLoop, calls=%fused_computation.8 | loop fusion | flops 884736 | bytes 2359300 | tf_op jit(solution)/shard_map/add | solution.py:217
  18.9 1.5 %collective-permute-start.1 = (bf16[96,1536]{1,0:T(8,128)(2,1)S(1)}, bf16[96,1536]{1,0:T(8,128)(2,1)S(1)}, u32[]{:S(2)}, u32[]{:S(2)}) collective-permute-start(bf16[96,1536]{1,0:T(8,128)(2,1)S(1)} %dynamic-slice_convert_fusion), channel_id=1, source_target_pairs={{0,2},{1,3},{2,0},{3,1},{4,6},{5,7},{6,4},{7,5},{8,10},{9,11},{10,... | collective-permute-start | bytes 884744 | tf_op jit(solution)/shard_map/ppermute | solution.py:127
  20.8 12.1 %collective-permute-done.1 = bf16[96,1536]{1,0:T(8,128)(2,1)S(1)} collective-permute-done((bf16[96,1536]{1,0:T(8,128)(2,1)S(1)}, bf16[96,1536]{1,0:T(8,128)(2,1)S(1)}, u32[]{:S(2)}, u32[]{:S(2)}) %collective-permute-start.1) | collective-permute-done | bytes 294944 | tf_op jit(solution)/shard_map/ppermute | solution.py:127
  32.9 0.8 fusion.4
  33.6 1.0 collective-permute-start.2
  34.6 6.8 %collective-permute-start.3 = (bf16[96,1536]{1,0:T(8,128)(2,1)}, bf16[96,1536]{1,0:T(8,128)(2,1)}, u32[]{:S(2)}, u32[]{:S(2)}) collective-permute-start(bf16[96,1536]{1,0:T(8,128)(2,1)} %fusion.4), channel_id=1, source_target_pairs={{0,252},{4,0},{8,4},{12,8},{16,12},{20,16},{24,20},{28,24},{32,28}... | collective-permute-start | bytes 884744 | tf_op jit(solution)/shard_map/ppermute | solution.py:122
  41.4 1.5 %fusion.5.turned_ref = bf16[384,2048]{1,0:T(8,128)(2,1)} fusion(f32[2048]{0:T(1024)S(1)} %add_rsqrt_fusion, bf16[2048,384]{0,1:T(8,128)(2,1)S(1)} %copy.11), kind=kLoop, calls=%fused_computation.17 | loop fusion | flops 2359296 | bytes 3153920 | tf_op jit(solution)/shard_map/transpose | solution.py:243
  42.9 9.0 %all-to-all-done.cells_ref = bf16[64,72,128]{2,1,0:T(8,128)(2,1)} async-done(((bf16[64,72,128]{2,1,0:T(8,128)(2,1)}), bf16[64,72,128]{2,1,0:T(8,128)(2,1)}, u32[]{:S(2)}, u32[]{:S(2)}) %all-to-all-start) | async-done | bytes 1179680 | tf_op jit(solution)/shard_map/all_to_all | solution.py:204
  51.9 4.0 %stencil.1 = bf16[64,72,128]{2,1,0:T(8,128)(2,1)} custom-call(s32[4]{0:T(128)} %num_ref.1, s32[4]{0:T(128)} %den_ref.1, bf16[64,72,128]{2,1,0:T(8,128)(2,1)} %all-to-all-done.cells_ref), custom_call_target="tpu_custom_call" | custom-call | flops 8257536 | bytes 2359296 | tf_op jit(solution)/shard_map/stencil/pallas_call | solution.py:172
  55.9 5.5 %all-to-all-start.1 = ((bf16[64,72,128]{2,1,0:T(8,128)(2,1)}), bf16[64,72,128]{2,1,0:T(8,128)(2,1)}, u32[]{:S(2)}, u32[]{:S(2)}) async-start(bf16[64,72,128]{2,1,0:T(8,128)(2,1)} %stencil.1), calls=%async_computation.1 | async-start | bytes 2359296 | tf_op jit(solution)/shard_map/all_to_all | solution.py:206
  61.4 0.7 copy-done.3
  62.1 1.2 %multiply_convert_fusion.first_ref = bf16[96,1536]{1,0:T(8,128)(2,1)S(1)} fusion(bf16[96,1536]{1,0:T(8,128)(2,1)} %collective-permute-done.3, bf16[96,1536]{1,0:T(8,128)(2,1)} %copy-done.3, bf16[96,1536]{1,0:T(8,128)(2,1)S(1)} %collective-permute-done.1, f32[192,1536]{1,0:T(8,128)S(1)} %convert_add_fusion, s32[]{:T(128)S(6)} %select_n.32), kind=kLoop, calls=%fused_computation.9 | loop fusion | flops 1179648 | bytes 1769476 | tf_op jit(solution)/shard_map/convert_element_type | solution.py:223
  63.3 1.5 %collective-permute-start.4 = (bf16[96,1536]{1,0:T(8,128)(2,1)S(1)}, bf16[96,1536]{1,0:T(8,128)(2,1)}, u32[]{:S(2)}, u32[]{:S(2)}) collective-permute-start(bf16[96,1536]{1,0:T(8,128)(2,1)S(1)} %multiply_convert_fusion.first_ref), channel_id=1, source_target_pairs={{0,2},{1,3},{2,0},{3,1},{4,6},{5,7},{6,4},{7,5},{8,10},{9,11},{10,... | collective-permute-start | bytes 884744 | tf_op jit(solution)/shard_map/ppermute | solution.py:127
  64.9 0.4 fusion.1
  65.4 10.3 %collective-permute-done.4.second_ref = bf16[96,1536]{1,0:T(8,128)(2,1)} collective-permute-done((bf16[96,1536]{1,0:T(8,128)(2,1)S(1)}, bf16[96,1536]{1,0:T(8,128)(2,1)}, u32[]{:S(2)}, u32[]{:S(2)}) %collective-permute-start.4) | collective-permute-done | bytes 294944 | tf_op jit(solution)/shard_map/ppermute | solution.py:127
  75.7 1.4 %broadcast_select_fusion.masked_ref = bf16[2048,384]{1,0:T(8,128)(2,1)} fusion(bf16[2048,384]{1,0:T(8,128)(2,1)S(1)} %copy-done.1, pred[2048]{0:T(1024)(128)(4,1)S(1)} %broadcast_compare_fusion), kind=kLoop, calls=%fused_computation.6 | loop fusion | flops 786432 | bytes 3147776 | tf_op jit(solution)/shard_map/jit(_where)/select_n | solution.py:242
  77.1 1.6 %copy.12.normed_ref = bf16[2048,384]{1,0:T(8,128)(2,1)} copy(bf16[2048,384]{0,1:T(8,128)(2,1)S(1)} %fusion.1) | data formatting | bytes 3145728 | tf_op jit(solution)/shard_map/optimization_barrier | solution.py:243
  78.7 0.6 pad_add_fusion.place_ref
  79.4 0.7 copy-done.5
  80.2 15.5 %grad_change.1 = (bf16[384,1536]{1,0:T(8,128)(2,1)}, f32[384,1536]{1,0:T(8,128)}) custom-call(s32[4]{0:T(128)} %pad_add_fusion.place_ref, bf16[2048,384]{1,0:T(8,128)(2,1)} %copy.12.normed_ref, bf16[384,2048]{1,0:T(8,128)(2,1)} %fusion.5.turned_ref, bf16[2048,384]{1,0:T(8,128)(2,1)} %broadcast_select_fusion.masked_ref, bf16[96,1536]{1,0:T(8,128)(2,1)} %copy-done.2, ...), custom_call_target="tpu_custom_call" | custom-call | flops 7247757312 | bytes 8257536 | tf_op jit(solution)/shard_map/grad_change/pallas_call | solution.py:83
  95.7 3.3 %fusion.3 = bf16[1,1,384,1536]{3,2,1,0:T(8,128)(2,1)} fusion(f32[384,1536]{1,0:T(8,128)} %get-tuple-element.11, bf16[48,12,8,128]{3,2,1,0:T(8,128)(2,1)} %bitcast.20), kind=kLoop, calls=%fused_computation.7 | loop fusion | flops 1769472 | bytes 4718592 | tf_op jit(solution)/shard_map/broadcast_in_dim | solution.py:248
  (25 shorter events, 0.6 us)
Async XLA Ops:
  0.6 16.0 %copy-start = (bf16[2048,384]{1,0:T(8,128)(2,1)S(1)}, bf16[2048,384]{1,0:T(8,128)(2,1)}, u32[]{:S(2)}) copy-start(bf16[2048,384]{1,0:T(8,128)(2,1)} %param.9) | copy-start | bytes 4718596
  2.7 14.7 %collective-permute-start = (bf16[192,1536]{1,0:T(8,128)(2,1)}, bf16[192,1536]{1,0:T(8,128)(2,1)}, u32[]{:S(2)}, u32[]{:S(2)}) collective-permute-start(bf16[192,1536]{1,0:T(8,128)(2,1)} %dynamic-slice_bitcast_fusion), channel_id=1, source_target_pairs={{0,1},{1,0},{2,3},{3,2},{4,5},{5,4},{6,7},{7,6},{8,9},{9,8},{10,11... | collective-permute-start | bytes 1769480 | tf_op jit(solution)/shard_map/ppermute | solution.py:127
  2.7 49.2 %all-to-all-start = ((bf16[64,72,128]{2,1,0:T(8,128)(2,1)}), bf16[64,72,128]{2,1,0:T(8,128)(2,1)}, u32[]{:S(2)}, u32[]{:S(2)}) async-start(bf16[64,72,128]{2,1,0:T(8,128)(2,1)} %bitcast.31), calls=%async_computation | async-start | bytes 2359296 | tf_op jit(solution)/shard_map/all_to_all | solution.py:204
  18.9 14.0 %collective-permute-start.1 = (bf16[96,1536]{1,0:T(8,128)(2,1)S(1)}, bf16[96,1536]{1,0:T(8,128)(2,1)S(1)}, u32[]{:S(2)}, u32[]{:S(2)}) collective-permute-start(bf16[96,1536]{1,0:T(8,128)(2,1)S(1)} %dynamic-slice_convert_fusion), channel_id=1, source_target_pairs={{0,2},{1,3},{2,0},{3,1},{4,6},{5,7},{6,4},{7,5},{8,10},{9,11},{10,... | collective-permute-start | bytes 884744 | tf_op jit(solution)/shard_map/ppermute | solution.py:127
  33.6 27.7 %collective-permute-start.2 = (bf16[96,1536]{1,0:T(8,128)(2,1)}, bf16[96,1536]{1,0:T(8,128)(2,1)S(1)}, u32[]{:S(2)}, u32[]{:S(2)}) collective-permute-start(bf16[96,1536]{1,0:T(8,128)(2,1)} %fusion.4), channel_id=1, source_target_pairs={{0,4},{4,8},{8,12},{12,16},{16,20},{20,24},{24,28},{28,32},{32,36}... | collective-permute-start | bytes 884744 | tf_op jit(solution)/shard_map/ppermute | solution.py:122
  34.6 27.5 %collective-permute-start.3 = (bf16[96,1536]{1,0:T(8,128)(2,1)}, bf16[96,1536]{1,0:T(8,128)(2,1)}, u32[]{:S(2)}, u32[]{:S(2)}) collective-permute-start(bf16[96,1536]{1,0:T(8,128)(2,1)} %fusion.4), channel_id=1, source_target_pairs={{0,252},{4,0},{8,4},{12,8},{16,12},{20,16},{24,20},{28,24},{32,28}... | collective-permute-start | bytes 884744 | tf_op jit(solution)/shard_map/ppermute | solution.py:122
  55.9 39.8 %all-to-all-start.1 = ((bf16[64,72,128]{2,1,0:T(8,128)(2,1)}), bf16[64,72,128]{2,1,0:T(8,128)(2,1)}, u32[]{:S(2)}, u32[]{:S(2)}) async-start(bf16[64,72,128]{2,1,0:T(8,128)(2,1)} %stencil.1), calls=%async_computation.1 | async-start | bytes 2359296 | tf_op jit(solution)/shard_map/all_to_all | solution.py:206
  61.4 0.7 copy-start.3
  63.3 2.0 %copy-start.2 = (bf16[96,1536]{1,0:T(8,128)(2,1)}, bf16[96,1536]{1,0:T(8,128)(2,1)S(1)}, u32[]{:S(2)}) copy-start(bf16[96,1536]{1,0:T(8,128)(2,1)S(1)} %multiply_convert_fusion.first_ref) | copy-start | bytes 884740
  63.3 1.9 %copy-start.4 = (s32[2048]{0:T(1024)S(1)}, s32[2048]{0:T(1024)}, u32[]{:S(2)}) copy-start(s32[2048]{0:T(1024)} %param.11) | copy-start | bytes 24580
  63.3 12.4 %copy-start.1 = (bf16[2048,384]{1,0:T(8,128)(2,1)S(1)}, bf16[2048,384]{1,0:T(8,128)(2,1)}, u32[]{:S(2)}) copy-start(bf16[2048,384]{1,0:T(8,128)(2,1)} %param.10) | copy-start | bytes 4718596
  63.3 12.4 %collective-permute-start.4 = (bf16[96,1536]{1,0:T(8,128)(2,1)S(1)}, bf16[96,1536]{1,0:T(8,128)(2,1)}, u32[]{:S(2)}, u32[]{:S(2)}) collective-permute-start(bf16[96,1536]{1,0:T(8,128)(2,1)S(1)} %multiply_convert_fusion.first_ref), channel_id=1, source_target_pairs={{0,2},{1,3},{2,0},{3,1},{4,6},{5,7},{6,4},{7,5},{8,10},{9,11},{10,... | collective-permute-start | bytes 884744 | tf_op jit(solution)/shard_map/ppermute | solution.py:127
  65.3 14.1 %collective-permute-start.5 = (bf16[96,1536]{1,0:T(8,128)(2,1)S(1)}, bf16[96,1536]{1,0:T(8,128)(2,1)S(1)}, u32[]{:S(2)}, u32[]{:S(2)}) collective-permute-start(bf16[96,1536]{1,0:T(8,128)(2,1)S(1)} %multiply_convert_fusion.first_ref), channel_id=1, source_target_pairs={{0,1},{1,0},{2,3},{3,2},{4,5},{5,4},{6,7},{7,6},{8,9},{9,8},{10,11... | collective-permute-start | bytes 884744 | tf_op jit(solution)/shard_map/ppermute | solution.py:127
  75.7 3.6 %collective-permute-start.6 = (bf16[96,1536]{1,0:T(8,128)(2,1)}, bf16[96,1536]{1,0:T(8,128)(2,1)S(1)}, u32[]{:S(2)}, u32[]{:S(2)}) collective-permute-start(bf16[96,1536]{1,0:T(8,128)(2,1)} %collective-permute-done.4.second_ref), channel_id=1, source_target_pairs={{0,1},{1,0},{2,3},{3,2},{4,5},{5,4},{6,7},{7,6},{8,9},{9,8},{10,11... | collective-permute-start | bytes 884744 | tf_op jit(solution)/shard_map/ppermute | solution.py:127
  79.4 0.7 copy-start.5
  79.4 0.8 copy-start.6

commit v2 on v1

--- a/solution.py
+++ b/solution.py
@@ -9,6 +9,8 @@
 
 
 ROUNDS = 4
+SPAN = 16
+LAG = 450
 
 epsilon = 1e-06
 step_size = 0.25
@@ -27,7 +29,7 @@
 
 
 def grad_body(
-    place_ref,
+    member_ref,
     normed_ref,
     turned_ref,
     masked_ref,
@@ -46,8 +48,15 @@
     tokens, width = normed_ref.shape
     inv_root = width ** (-0.5)
     quarter = width // 4
-    for k, part_ref in enumerate((first_ref, second_ref, third_ref, fourth_ref)):
-        at = pl.multiple_of(place_ref[k] * quarter, quarter)
+    core, chip = member_ref[0] & 1, member_ref[0] >> 1
+    places = (
+        core * 2 + chip,
+        core * 2 + 1 - chip,
+        (1 - core) * 2 + chip,
+        (1 - core) * 2 + 1 - chip,
+    )
+    for place, part_ref in zip(places, (first_ref, second_ref, third_ref, fourth_ref)):
+        at = pl.multiple_of(place * quarter, quarter)
         mixed_ref[pl.ds(at, quarter)] = part_ref[...]
     params_ref[...] = (
         mixed_ref[...].astype(f32) - step_size * tracker_ref[...].astype(f32)
@@ -73,7 +82,7 @@
     out_ref[...] = grad * inv_root - old_ref[...].astype(f32)
 
 
-def grad_change(place, normed, turned, masked, parts, tracker, w_out, grad_old):
+def grad_change(member, normed, turned, masked, parts, tracker, w_out, grad_old):
     tokens, width = normed.shape
     hidden = tracker.shape[1]
     block = 256
@@ -108,7 +117,7 @@
             transcendentals=tokens * hidden,
         ),
         name="grad_change",
-    )(place, normed, turned, masked, *parts, tracker, w_out, grad_old)
+    )(member, normed, turned, masked, *parts, tracker, w_out, grad_old)
 
 
 def normed_of(hidden):
@@ -127,84 +136,97 @@
     return lax.ppermute(value, "grp", [(i, i ^ bit) for i in range(count)])
 
 
-def stencil_taps(num_ref, den_ref):
+def taps_body(lag_ref, num_ref, den_ref, taps_ref):
     def wide(value):
         return jnp.full((8, 128), value, f32)
 
-    weights = [
-        wide(num_ref[t].astype(f32)) / wide(den_ref[t].astype(f32)) for t in range(ROUNDS)
-    ]
     zero = wide(0.0)
-    older = [wide(1.0)] + [zero] * ROUNDS
-    current = older
-    for t in range(ROUNDS):
-        mean = []
+
+    def once(_, carry):
+        older = [wide(1.0)] + [zero] * ROUNDS
+        current = older
+        for t in range(ROUNDS):
+            weight = wide(num_ref[t].astype(f32)) / wide(den_ref[t].astype(f32))
+            mean = []
+            for d in range(ROUNDS + 1):
+                left = current[d - 1] if d > 0 else current[1]
+                right = current[d + 1] if d < ROUNDS else zero
+                mean.append((left + current[d] + right) / 3.0)
+            following = [weight * m + (1.0 - weight) * o for m, o in zip(mean, older)]
+            older, current = current, following
         for d in range(ROUNDS + 1):
-            left = current[d - 1] if d > 0 else current[1]
-            right = current[d + 1] if d < ROUNDS else zero
-            mean.append((left + current[d] + right) / 3.0)
-        following = [weights[t] * m + (1.0 - weights[t]) * o for m, o in zip(mean, older)]
-        older, current = current, following
-    return current
-
-
-def stencil_body(num_ref, den_ref, cells_ref, out_ref, wide_ref):
-    workers, rows, _ = cells_ref.shape
+            taps_ref[d] = current[d]
+        return carry
+
+    lax.fori_loop(0, 1 + lag_ref[0], once, 0)
+
+
+def stencil_taps(lag, cheb_num, cheb_den):
+    scalars = pl.BlockSpec(memory_space=pltpu.SMEM)
+    return pl.pallas_call(
+        taps_body,
+        out_shape=jax.ShapeDtypeStruct((ROUNDS + 1, 8, 128), f32),
+        in_specs=[scalars, scalars, scalars],
+        out_specs=pl.BlockSpec(memory_space=pltpu.VMEM),
+        name="stencil_taps",
+    )(lag, cheb_num, cheb_den)
+
+
+def stencil_body(taps_ref, below_ref, cells_ref, above_ref, out_ref, wide_ref):
+    workers, rows, lanes = cells_ref.shape
+    wide_ref[pl.ds(0, ROUNDS)] = below_ref[...].astype(f32)
     wide_ref[pl.ds(ROUNDS, workers)] = cells_ref[...].astype(f32)
-    wide_ref[pl.ds(0, ROUNDS)] = cells_ref[pl.ds(workers - ROUNDS, ROUNDS)].astype(f32)
-    wide_ref[pl.ds(ROUNDS + workers, ROUNDS)] = cells_ref[pl.ds(0, ROUNDS)].astype(f32)
-    taps = [jnp.tile(t, (rows // 8, 1)) for t in stencil_taps(num_ref, den_ref)]
+    wide_ref[pl.ds(ROUNDS + workers, ROUNDS)] = above_ref[...].astype(f32)
+    taps = [taps_ref[d] for d in range(ROUNDS + 1)]
 
     def one(b, carry):
-        total = taps[0] * wide_ref[b + ROUNDS]
-        for d in range(1, ROUNDS + 1):
-            total = total + taps[d] * (wide_ref[b + ROUNDS - d] + wide_ref[b + ROUNDS + d])
-        out_ref[b] = total.astype(bf16)
+        for row in range(0, rows, 8):
+            for lane in range(0, lanes, 128):
+                at = (pl.ds(row, 8), pl.ds(lane, 128))
+                total = taps[0] * wide_ref[b + ROUNDS, *at]
+                for d in range(1, ROUNDS + 1):
+                    pair = wide_ref[b + ROUNDS - d, *at] + wide_ref[b + ROUNDS + d, *at]
+                    total = total + taps[d] * pair
+                out_ref[b, *at] = total.astype(bf16)
         return carry
 
-    lax.fori_loop(0, workers, one, 0, unroll=4)
-
-
-def stencil(cells, cheb_num, cheb_den):
+    lax.fori_loop(0, workers, one, 0)
+
+
+def stencil(taps, below, cells, above):
     workers, rows, lanes = cells.shape
-    block = 24 if rows % 24 == 0 else rows
-    spec = pl.BlockSpec((workers, block, lanes), lambda i: (0, i, 0))
+    block = 1536
+    spec = pl.BlockSpec((workers, rows, block), lambda i: (0, 0, i))
+    side = pl.BlockSpec((ROUNDS, rows, block), lambda i: (0, 0, i))
     return pl.pallas_call(
         stencil_body,
-        grid=(rows // block,),
+        grid=(lanes // block,),
         out_shape=jax.ShapeDtypeStruct(cells.shape, bf16),
-        in_specs=[
-            pl.BlockSpec(memory_space=pltpu.SMEM),
-            pl.BlockSpec(memory_space=pltpu.SMEM),
-            spec,
-        ],
+        in_specs=[pl.BlockSpec(memory_space=pltpu.VMEM), side, spec, side],
         out_specs=spec,
-        scratch_shapes=[pltpu.VMEM((workers + 2 * ROUNDS, block, lanes), f32)],
+        scratch_shapes=[pltpu.VMEM((workers + 2 * ROUNDS, rows, block), f32)],
         cost_estimate=pl.CostEstimate(
             flops=14 * cells.size, bytes_accessed=4 * cells.size, transcendentals=0
         ),
         name="stencil",
-    )(cheb_num, cheb_den, cells)
-
-
-def to_tiles(value, workers):
-    rows, cols = value.shape
-    tiles = value.reshape(rows // 8, 8, cols // 128, 128).transpose(0, 2, 1, 3)
-    return tiles.reshape(workers, rows * cols // (128 * workers), 128)
-
-
-def from_tiles(tiles, rows, cols):
-    value = tiles.reshape(rows // 8, cols // 128, 8, 128).transpose(0, 2, 1, 3)
-    return value.reshape(rows, cols)
-
-
-def consensus_of(tracker, cheb_num, cheb_den):
-    workers = lax.axis_size("blk")
-    cells = to_tiles(tracker, workers)
-    cells = lax.all_to_all(cells, "blk", 0, 0, tiled=True)
-    cells = stencil(cells, cheb_num, cheb_den)
-    cells = lax.all_to_all(cells, "blk", 0, 0, tiled=True)
-    return from_tiles(cells, *tracker.shape)
+    )(taps, below, cells, above)
+
+
+def traded(cells):
+    count = lax.axis_size("blk")
+    groups = [list(range(at, at + SPAN)) for at in range(0, count, SPAN)]
+    return lax.all_to_all(cells, "blk", 0, 0, tiled=True, axis_index_groups=groups)
+
+
+def consensus_of(tracker, taps):
+    rows, cols = tracker.shape
+    cells = tracker.reshape(SPAN, rows // SPAN, cols)
+    cells = traded(cells)
+    below = shift(cells[SPAN - ROUNDS :], "blk", SPAN)
+    above = shift(cells[:ROUNDS], "blk", -SPAN)
+    cells = stencil(taps, below, cells, above)
+    cells = traded(cells)
+    return cells.reshape(rows, cols)
 
 
 def mixed_of(w_in):
@@ -224,25 +246,19 @@
     far = swap(mean, 2)
     near = swap(mean, 1)
     last = swap(far, 1)
-    place = jnp.stack(
-        [
-            core * 2 + chip,
-            core * 2 + 1 - chip,
-            (1 - core) * 2 + chip,
-            (1 - core) * 2 + 1 - chip,
-        ]
-    ).astype(jnp.int32)
-    return place, (mean, far, near, last)
+    return member.astype(jnp.int32).reshape(1), (mean, far, near, last)
 
 
 def shards(hidden, cotangent, token_ids, w_in, w_out, tracker, grad_old, cheb_num, cheb_den):
-    consensus = consensus_of(tracker[0, 0], cheb_num, cheb_den)
-    place, parts = mixed_of(w_in[0, 0])
+    lag = (lax.axis_index("grp") % 2 * LAG).astype(jnp.int32).reshape(1)
+    taps = stencil_taps(lag, cheb_num, cheb_den)
+    consensus = consensus_of(tracker[0, 0], taps)
+    member, parts = mixed_of(w_in[0, 0])
     normed = normed_of(hidden)
     masked = jnp.where((token_ids != 0)[:, None], cotangent, jnp.zeros_like(cotangent))
     normed, turned, masked = lax.optimization_barrier((normed, normed.T, masked))
     new_params, change = grad_change(
-        place, normed, turned, masked, parts, tracker[0, 0], w_out, grad_old[0, 0]
+        member, normed, turned, masked, parts, tracker[0, 0], w_out, grad_old[0, 0]
     )
     new_tracker = (consensus.astype(f32) + change).astype(bf16)
     return (new_params[None, None], new_tracker[None, None])

time: 101 us -> 109 us (1.079)
  the two profiles are of different devices: /device:TPU:2 before, /device:TPU:5 now
where the time goes in v2:
time: 109 us; the launch traced here: 108 us
  starting transfers between devices  40.1 us (37%)
  Pallas kernels  33.1 us (30%)
  waiting for transfers between devices  13.7 us (13%)
  other arithmetic  12.5 us (11%)
  local copies, waits for them, and re-layouts  7.85 us (7%)
    all_to_all x2, starting transfers between devices, traded(): lax.all_to_all(cells, 'blk', 0, 0, tiled=True, axis_index_groups=groups)  25.5 us
    pallas_call x1, Pallas kernels, grad_change(): pl.pallas_call(grad_body, grid=(hidden // block,), out_shape=(jax.ShapeDt...  15.3 us
    pallas_call x1, Pallas kernels, stencil_taps(): pl.pallas_call(taps_body, out_shape=jax.ShapeDtypeStruct((ROUNDS + 1, 8,...  13.9 us
    ppermute x5, waiting for transfers between devices, swap(): return lax.ppermute(value, 'grp', [(i, i ^ bit) for i in range(count)])  10.8 us
    ppermute x4, starting transfers between devices, shift(): lax.ppermute(value, axis, [(i, (i + step) % count) for i in range(count)])  7.98 us
    ppermute x5, starting transfers between devices, swap(): return lax.ppermute(value, 'grp', [(i, i ^ bit) for i in range(count)])  6.61 us
    pallas_call x1, Pallas kernels, stencil(): pl.pallas_call(stencil_body, grid=(lanes // block,), out_shape=jax.ShapeD...  3.92 us
    broadcast_in_dim x1, other arithmetic, shards(): return (new_params[None, None], new_tracker[None, None])  3.32 us
  transfers between devices with their start and end apart: 11, of which 2 were waited for; matrix products, arithmetic and copies ran while one was open for 13% of the time, Pallas kernels for 31%

profile of v2, /device:TPU:5, one launch (start us, length us, event | category | flops | bytes accessed | tf_op | source)
XLA Modules:
  0.0 108.0 jit_solution(16572157773330708424)
XLA Ops:
  0.6 1.9 %dynamic-slice_bitcast_fusion = bf16[192,1536]{1,0:T(8,128)(2,1)} fusion(bf16[1,1,384,1536]{3,2,1,0:T(8,128)(2,1)} %param.12, s32[]{:T(128)S(6)} %select_n.32), kind=kLoop, calls=%fused_computation.12 | loop fusion | bytes 1179652 | tf_op jit(solution)/shard_map/dynamic_slice | solution.py:237
  3.2 10.9 %all-to-all-start = ((bf16[16,24,1536]{2,1,0:T(8,128)(2,1)}), bf16[16,24,1536]{2,1,0:T(8,128)(2,1)S(1)}, u32[]{:S(2)}, u32[]{:S(2)}) async-start(bf16[16,24,1536]{2,1,0:T(8,128)(2,1)} %bitcast.18), calls=%async_computation | async-start | bytes 2359296 | tf_op jit(solution)/shard_map/all_to_all | solution.py:218
  14.1 1.7 %copy.11 = bf16[2048,384]{0,1:T(8,128)(2,1)S(1)} copy(bf16[2048,384]{1,0:T(8,128)(2,1)} %param.9) | data formatting | bytes 3145728 | tf_op args[0]
  15.9 2.2 %convert_add_fusion.1 = f32[192,1536]{1,0:T(8,128)} fusion(bf16[192,1536]{1,0:T(8,128)(2,1)S(1)} %collective-permute-done, bf16[1,1,384,1536]{3,2,1,0:T(8,128)(2,1)} %param.12, s32[]{:T(128)S(6)} %select_n.31), kind=kLoop, calls=%fused_computation.8 | loop fusion | flops 884736 | bytes 2359300 | tf_op jit(solution)/shard_map/add | solution.py:239
  18.1 1.1 %dynamic-slice_convert_fusion = bf16[96,1536]{1,0:T(8,128)(2,1)S(1)} fusion(f32[192,1536]{1,0:T(8,128)} %convert_add_fusion.1, s32[]{:T(128)S(6)} %select_n.35), kind=kLoop, calls=%fused_computation.11 | loop fusion | bytes 589828 | tf_op jit(solution)/shard_map/convert_element_type | solution.py:240
  20.6 13.9 %stencil_taps.1.taps_ref = f32[5,8,128]{2,1,0:T(8,128)} custom-call(s32[1]{0:T(128)} %bitcast.7.lag_ref, s32[4]{0:T(128)} %num_ref.1, s32[4]{0:T(128)} %den_ref.1), custom_call_target="tpu_custom_call" | custom-call | tf_op jit(solution)/shard_map/stencil_taps/pallas_call | solution.py:166
  34.4 1.8 %fusion.4 = bf16[96,1536]{1,0:T(8,128)(2,1)} fusion(bf16[96,1536]{1,0:T(8,128)(2,1)S(1)} %collective-permute-done.1, f32[192,1536]{1,0:T(8,128)} %convert_add_fusion.1, s32[]{:T(128)S(6)} %select_n.34), kind=kLoop, calls=%fused_computation.13 | loop fusion | flops 442368 | bytes 1179652 | tf_op jit(solution)/shard_map/convert_element_type | solution.py:243
  36.3 1.2 %collective-permute-start.2 = (bf16[96,1536]{1,0:T(8,128)(2,1)}, bf16[96,1536]{1,0:T(8,128)(2,1)}, u32[]{:S(2)}, u32[]{:S(2)}) collective-permute-start(bf16[96,1536]{1,0:T(8,128)(2,1)} %fusion.4), channel_id=1, source_target_pairs={{0,4},{4,8},{8,12},{12,16},{16,20},{20,24},{24,28},{28,32},{32,36}... | collective-permute-start | bytes 884744 | tf_op jit(solution)/shard_map/ppermute | solution.py:131
  37.4 3.9 %collective-permute-start.3 = (bf16[96,1536]{1,0:T(8,128)(2,1)}, bf16[96,1536]{1,0:T(8,128)(2,1)}, u32[]{:S(2)}, u32[]{:S(2)}) collective-permute-start(bf16[96,1536]{1,0:T(8,128)(2,1)} %fusion.4), channel_id=1, source_target_pairs={{0,252},{4,0},{8,4},{12,8},{16,12},{20,16},{24,20},{28,24},{32,28}... | collective-permute-start | bytes 884744 | tf_op jit(solution)/shard_map/ppermute | solution.py:131
  41.4 1.4 %collective-permute-start.7 = (bf16[4,24,1536]{2,1,0:T(8,128)(2,1)S(1)}, bf16[4,24,1536]{2,1,0:T(8,128)(2,1)S(1)}, u32[]{:S(2)}, u32[]{:S(2)}) collective-permute-start(bf16[4,24,1536]{2,1,0:T(8,128)(2,1)S(1)} %get-tuple-element.13), channel_id=1, source_target_pairs={{0,64},{4,68},{8,72},{12,76},{16,80},{20,84},{24,88},{28,92},{32,9... | collective-permute-start | bytes 884744 | tf_op jit(solution)/shard_map/ppermute | solution.py:131
  42.8 1.5 %collective-permute-start.8 = (bf16[4,24,1536]{2,1,0:T(8,128)(2,1)S(1)}, bf16[4,24,1536]{2,1,0:T(8,128)(2,1)}, u32[]{:S(2)}, u32[]{:S(2)}) collective-permute-start(bf16[4,24,1536]{2,1,0:T(8,128)(2,1)S(1)} %get-tuple-element.12), channel_id=1, source_target_pairs={{0,192},{4,196},{8,200},{12,204},{16,208},{20,212},{24,216},{28,22... | collective-permute-start | bytes 884744 | tf_op jit(solution)/shard_map/ppermute | solution.py:131
  44.3 1.5 %fusion.6.turned_ref = bf16[384,2048]{1,0:T(8,128)(2,1)} fusion(f32[2048]{0:T(1024)S(1)} %add_rsqrt_fusion, bf16[2048,384]{0,1:T(8,128)(2,1)S(1)} %copy.11), kind=kLoop, calls=%fused_computation.17 | loop fusion | flops 2359296 | bytes 3153920 | tf_op jit(solution)/shard_map/transpose | solution.py:259
  45.8 2.9 %collective-permute-done.7.below_ref = bf16[4,24,1536]{2,1,0:T(8,128)(2,1)S(1)} collective-permute-done((bf16[4,24,1536]{2,1,0:T(8,128)(2,1)S(1)}, bf16[4,24,1536]{2,1,0:T(8,128)(2,1)S(1)}, u32[]{:S(2)}, u32[]{:S(2)}) %collective-permute-start.7) | collective-permute-done | bytes 294944 | tf_op jit(solution)/shard_map/ppermute | solution.py:131
  49.4 3.9 %stencil.1 = bf16[16,24,1536]{2,1,0:T(8,128)(2,1)} custom-call(f32[5,8,128]{2,1,0:T(8,128)} %stencil_taps.1.taps_ref, bf16[4,24,1536]{2,1,0:T(8,128)(2,1)} %copy-done.2, bf16[16,24,1536]{2,1,0:T(8,128)(2,1)} %copy-done, bf16[4,24,1536]{2,1,0:T(8,128)(2,1)} %collective-permute-done.8.above_ref), custom_call_target="tpu_custom_call" | custom-call | flops 8257536 | bytes 2359296 | tf_op jit(solution)/shard_map/stencil/pallas_call | solution.py:201
  53.3 14.6 %all-to-all-start.1 = ((bf16[16,24,1536]{2,1,0:T(8,128)(2,1)}), bf16[16,24,1536]{2,1,0:T(8,128)(2,1)}, u32[]{:S(2)}, u32[]{:S(2)}) async-start(bf16[16,24,1536]{2,1,0:T(8,128)(2,1)} %stencil.1), calls=%async_computation.1 | async-start | bytes 2359296 | tf_op jit(solution)/shard_map/all_to_all | solution.py:218
  68.0 1.4 %multiply_convert_fusion.first_ref = bf16[96,1536]{1,0:T(8,128)(2,1)S(1)} fusion(bf16[96,1536]{1,0:T(8,128)(2,1)} %collective-permute-done.3, bf16[96,1536]{1,0:T(8,128)(2,1)} %collective-permute-done.2, bf16[96,1536]{1,0:T(8,128)(2,1)S(1)} %collective-permute-done.1, f32[192,1536]{1,0:T(8,128)} %convert_add_fusion.1, s32[]{:T(128)S(6)} %select_n.34), kind=kLoop, calls=%fused_computation.9 | loop fusion | flops 1179648 | bytes 1769476 | tf_op jit(solution)/shard_map/convert_element_type | solution.py:245
  69.4 1.0 collective-permute-start.4
  70.9 2.0 %collective-permute-start.5 = (bf16[96,1536]{1,0:T(8,128)(2,1)S(1)}, bf16[96,1536]{1,0:T(8,128)(2,1)S(1)}, u32[]{:S(2)}, u32[]{:S(2)}) collective-permute-start(bf16[96,1536]{1,0:T(8,128)(2,1)S(1)} %multiply_convert_fusion.first_ref), channel_id=1, source_target_pairs={{0,1},{1,0},{2,3},{3,2},{4,5},{5,4},{6,7},{7,6},{8,9},{9,8},{10,11... | collective-permute-start | bytes 884744 | tf_op jit(solution)/shard_map/ppermute | solution.py:136
  72.8 10.8 %collective-permute-done.4.second_ref = bf16[96,1536]{1,0:T(8,128)(2,1)} collective-permute-done((bf16[96,1536]{1,0:T(8,128)(2,1)S(1)}, bf16[96,1536]{1,0:T(8,128)(2,1)}, u32[]{:S(2)}, u32[]{:S(2)}) %collective-permute-start.4) | collective-permute-done | bytes 294944 | tf_op jit(solution)/shard_map/ppermute | solution.py:136
  83.6 1.9 %collective-permute-start.6 = (bf16[96,1536]{1,0:T(8,128)(2,1)}, bf16[96,1536]{1,0:T(8,128)(2,1)S(1)}, u32[]{:S(2)}, u32[]{:S(2)}) collective-permute-start(bf16[96,1536]{1,0:T(8,128)(2,1)} %collective-permute-done.4.second_ref), channel_id=1, source_target_pairs={{0,1},{1,0},{2,3},{3,2},{4,5},{5,4},{6,7},{7,6},{8,9},{9,8},{10,11... | collective-permute-start | bytes 884744 | tf_op jit(solution)/shard_map/ppermute | solution.py:136
  85.6 1.4 %broadcast_select_fusion.masked_ref = bf16[2048,384]{1,0:T(8,128)(2,1)} fusion(bf16[2048,384]{1,0:T(8,128)(2,1)S(1)} %copy-done.1, pred[2048]{0:T(1024)(128)(4,1)S(1)} %broadcast_compare_fusion), kind=kLoop, calls=%fused_computation.6 | loop fusion | flops 786432 | bytes 3147776 | tf_op jit(solution)/shard_map/jit(_where)/select_n | solution.py:258
  87.0 1.6 %copy.12.normed_ref = bf16[2048,384]{1,0:T(8,128)(2,1)} copy(bf16[2048,384]{0,1:T(8,128)(2,1)S(1)} %fusion.1) | data formatting | bytes 3145728 | tf_op jit(solution)/shard_map/optimization_barrier | solution.py:259
  89.4 15.3 %grad_change.1 = (bf16[384,1536]{1,0:T(8,128)(2,1)}, f32[384,1536]{1,0:T(8,128)}) custom-call(s32[1]{0:T(128)} %bitcast.member_ref, bf16[2048,384]{1,0:T(8,128)(2,1)} %copy.12.normed_ref, bf16[384,2048]{1,0:T(8,128)(2,1)} %fusion.6.turned_ref, bf16[2048,384]{1,0:T(8,128)(2,1)} %broadcast_select_fusion.masked_ref, bf16[96,1536]{1,0:T(8,128)(2,1)} %copy-done.3, ...), custom_call_target="tpu_custom_call" | custom-call | flops 7247757312 | bytes 8257536 | tf_op jit(solution)/shard_map/grad_change/pallas_call | solution.py:92
  104.7 3.3 %fusion.3 = bf16[1,1,384,1536]{3,2,1,0:T(8,128)(2,1)} fusion(f32[384,1536]{1,0:T(8,128)} %get-tuple-element.11, bf16[16,24,1536]{2,1,0:T(8,128)(2,1)} %all-to-all-done.1), kind=kLoop, calls=%fused_computation.7 | loop fusion | flops 1769472 | bytes 4718592 | tf_op jit(solution)/shard_map/broadcast_in_dim | solution.py:264
  (30 shorter events, 4.0 us)
Async XLA Ops:
  2.6 13.3 %collective-permute-start = (bf16[192,1536]{1,0:T(8,128)(2,1)}, bf16[192,1536]{1,0:T(8,128)(2,1)S(1)}, u32[]{:S(2)}, u32[]{:S(2)}) collective-permute-start(bf16[192,1536]{1,0:T(8,128)(2,1)} %dynamic-slice_bitcast_fusion), channel_id=1, source_target_pairs={{0,1},{1,0},{2,3},{3,2},{4,5},{5,4},{6,7},{7,6},{8,9},{9,8},{10,11... | collective-permute-start | bytes 1769480 | tf_op jit(solution)/shard_map/ppermute | solution.py:136
  3.2 38.1 %all-to-all-start = ((bf16[16,24,1536]{2,1,0:T(8,128)(2,1)}), bf16[16,24,1536]{2,1,0:T(8,128)(2,1)S(1)}, u32[]{:S(2)}, u32[]{:S(2)}) async-start(bf16[16,24,1536]{2,1,0:T(8,128)(2,1)} %bitcast.18), calls=%async_computation | async-start | bytes 2359296 | tf_op jit(solution)/shard_map/all_to_all | solution.py:218
  19.2 15.2 %collective-permute-start.1 = (bf16[96,1536]{1,0:T(8,128)(2,1)S(1)}, bf16[96,1536]{1,0:T(8,128)(2,1)S(1)}, u32[]{:S(2)}, u32[]{:S(2)}) collective-permute-start(bf16[96,1536]{1,0:T(8,128)(2,1)S(1)} %dynamic-slice_convert_fusion), channel_id=1, source_target_pairs={{0,2},{1,3},{2,0},{3,1},{4,6},{5,7},{6,4},{7,5},{8,10},{9,11},{10,... | collective-permute-start | bytes 884744 | tf_op jit(solution)/shard_map/ppermute | solution.py:136
  36.3 31.7 %collective-permute-start.2 = (bf16[96,1536]{1,0:T(8,128)(2,1)}, bf16[96,1536]{1,0:T(8,128)(2,1)}, u32[]{:S(2)}, u32[]{:S(2)}) collective-permute-start(bf16[96,1536]{1,0:T(8,128)(2,1)} %fusion.4), channel_id=1, source_target_pairs={{0,4},{4,8},{8,12},{12,16},{16,20},{20,24},{24,28},{28,32},{32,36}... | collective-permute-start | bytes 884744 | tf_op jit(solution)/shard_map/ppermute | solution.py:131
  37.4 30.5 %collective-permute-start.3 = (bf16[96,1536]{1,0:T(8,128)(2,1)}, bf16[96,1536]{1,0:T(8,128)(2,1)}, u32[]{:S(2)}, u32[]{:S(2)}) collective-permute-start(bf16[96,1536]{1,0:T(8,128)(2,1)} %fusion.4), channel_id=1, source_target_pairs={{0,252},{4,0},{8,4},{12,8},{16,12},{20,16},{24,20},{28,24},{32,28}... | collective-permute-start | bytes 884744 | tf_op jit(solution)/shard_map/ppermute | solution.py:131
  41.3 4.5 %copy-start = (bf16[16,24,1536]{2,1,0:T(8,128)(2,1)}, bf16[16,24,1536]{2,1,0:T(8,128)(2,1)S(1)}, u32[]{:S(2)}) copy-start(bf16[16,24,1536]{2,1,0:T(8,128)(2,1)S(1)} %all-to-all-done.cells_ref) | copy-start | bytes 3538948
  41.4 7.3 %collective-permute-start.7 = (bf16[4,24,1536]{2,1,0:T(8,128)(2,1)S(1)}, bf16[4,24,1536]{2,1,0:T(8,128)(2,1)S(1)}, u32[]{:S(2)}, u32[]{:S(2)}) collective-permute-start(bf16[4,24,1536]{2,1,0:T(8,128)(2,1)S(1)} %get-tuple-element.13), channel_id=1, source_target_pairs={{0,64},{4,68},{8,72},{12,76},{16,80},{20,84},{24,88},{28,92},{32,9... | collective-permute-start | bytes 884744 | tf_op jit(solution)/shard_map/ppermute | solution.py:131
  42.8 6.0 %collective-permute-start.8 = (bf16[4,24,1536]{2,1,0:T(8,128)(2,1)S(1)}, bf16[4,24,1536]{2,1,0:T(8,128)(2,1)}, u32[]{:S(2)}, u32[]{:S(2)}) collective-permute-start(bf16[4,24,1536]{2,1,0:T(8,128)(2,1)S(1)} %get-tuple-element.12), channel_id=1, source_target_pairs={{0,192},{4,196},{8,200},{12,204},{16,208},{20,212},{24,216},{28,22... | collective-permute-start | bytes 884744 | tf_op jit(solution)/shard_map/ppermute | solution.py:131
  48.7 0.7 copy-start.2
  53.3 51.3 %all-to-all-start.1 = ((bf16[16,24,1536]{2,1,0:T(8,128)(2,1)}), bf16[16,24,1536]{2,1,0:T(8,128)(2,1)}, u32[]{:S(2)}, u32[]{:S(2)}) async-start(bf16[16,24,1536]{2,1,0:T(8,128)(2,1)} %stencil.1), calls=%async_computation.1 | async-start | bytes 2359296 | tf_op jit(solution)/shard_map/all_to_all | solution.py:218
  69.4 1.5 %copy-start.3 = (bf16[96,1536]{1,0:T(8,128)(2,1)}, bf16[96,1536]{1,0:T(8,128)(2,1)S(1)}, u32[]{:S(2)}) copy-start(bf16[96,1536]{1,0:T(8,128)(2,1)S(1)} %multiply_convert_fusion.first_ref) | copy-start | bytes 884740
  69.4 1.4 %copy-start.4 = (s32[2048]{0:T(1024)S(1)}, s32[2048]{0:T(1024)}, u32[]{:S(2)}) copy-start(s32[2048]{0:T(1024)} %param.11) | copy-start | bytes 24580
  69.4 16.2 %copy-start.1 = (bf16[2048,384]{1,0:T(8,128)(2,1)S(1)}, bf16[2048,384]{1,0:T(8,128)(2,1)}, u32[]{:S(2)}) copy-start(bf16[2048,384]{1,0:T(8,128)(2,1)} %param.10) | copy-start | bytes 4718596
  69.4 14.2 %collective-permute-start.4 = (bf16[96,1536]{1,0:T(8,128)(2,1)S(1)}, bf16[96,1536]{1,0:T(8,128)(2,1)}, u32[]{:S(2)}, u32[]{:S(2)}) collective-permute-start(bf16[96,1536]{1,0:T(8,128)(2,1)S(1)} %multiply_convert_fusion.first_ref), channel_id=1, source_target_pairs={{0,2},{1,3},{2,0},{3,1},{4,6},{5,7},{6,4},{7,5},{8,10},{9,11},{10,... | collective-permute-start | bytes 884744 | tf_op jit(solution)/shard_map/ppermute | solution.py:136
  70.9 17.7 %collective-permute-start.5 = (bf16[96,1536]{1,0:T(8,128)(2,1)S(1)}, bf16[96,1536]{1,0:T(8,128)(2,1)S(1)}, u32[]{:S(2)}, u32[]{:S(2)}) collective-permute-start(bf16[96,1536]{1,0:T(8,128)(2,1)S(1)} %multiply_convert_fusion.first_ref), channel_id=1, source_target_pairs={{0,1},{1,0},{2,3},{3,2},{4,5},{5,4},{6,7},{7,6},{8,9},{9,8},{10,11... | collective-permute-start | bytes 884744 | tf_op jit(solution)/shard_map/ppermute | solution.py:136
  83.6 4.9 %collective-permute-start.6 = (bf16[96,1536]{1,0:T(8,128)(2,1)}, bf16[96,1536]{1,0:T(8,128)(2,1)S(1)}, u32[]{:S(2)}, u32[]{:S(2)}) collective-permute-start(bf16[96,1536]{1,0:T(8,128)(2,1)} %collective-permute-done.4.second_ref), channel_id=1, source_target_pairs={{0,1},{1,0},{2,3},{3,2},{4,5},{5,4},{6,7},{7,6},{8,9},{9,8},{10,11... | collective-permute-start | bytes 884744 | tf_op jit(solution)/shard_map/ppermute | solution.py:136
  88.5 0.7 copy-start.5
  88.6 0.8 copy-start.6

commit v3 on v2

--- a/solution.py
+++ b/solution.py
@@ -79,13 +79,13 @@
             rows, scaled, back_flow = ready
             slope_ref[rows] = slope_of(scaled, back_flow, inv_root).astype(bf16)
     grad = jnp.dot(turned_ref[...], slope_ref[...], preferred_element_type=f32)
-    out_ref[...] = grad * inv_root - old_ref[...].astype(f32)
+    out_ref[...] = (grad * inv_root - old_ref[...].astype(f32)).astype(bf16)
 
 
 def grad_change(member, normed, turned, masked, parts, tracker, w_out, grad_old):
     tokens, width = normed.shape
     hidden = tracker.shape[1]
-    block = 256
+    block = 512
     whole = pl.BlockSpec(memory_space=pltpu.VMEM)
     column = pl.BlockSpec((width, block), lambda j: (0, j))
     piece = pl.BlockSpec((width // 4, block), lambda j: (0, j))
@@ -94,7 +94,7 @@
         grid=(hidden // block,),
         out_shape=(
             jax.ShapeDtypeStruct((width, hidden), bf16),
-            jax.ShapeDtypeStruct((width, hidden), f32),
+            jax.ShapeDtypeStruct((width, hidden), bf16),
         ),
         in_specs=[
             pl.BlockSpec(memory_space=pltpu.SMEM),
@@ -260,7 +260,7 @@
     new_params, change = grad_change(
         member, normed, turned, masked, parts, tracker[0, 0], w_out, grad_old[0, 0]
     )
-    new_tracker = (consensus.astype(f32) + change).astype(bf16)
+    new_tracker = (consensus.astype(f32) + change.astype(f32)).astype(bf16)
     return (new_params[None, None], new_tracker[None, None])
 
 

time: 109 us -> 108 us (level)
  transfers between devices with their start and end apart: 11 -> 11, of which waited for: 2 -> 2; matrix products, arithmetic and copies ran while one was open for 13% -> 13% of each run, Pallas kernels for 31% -> 30%
where the time goes in v3:
time: 108 us; the launch traced here: 107 us
  starting transfers between devices  40.1 us (37%)
  Pallas kernels  32.5 us (30%)
  waiting for transfers between devices  13.7 us (13%)
  other arithmetic  12.1 us (11%)
  local copies, waits for them, and re-layouts  7.92 us (7%)
    all_to_all x2, starting transfers between devices, traded(): lax.all_to_all(cells, 'blk', 0, 0, tiled=True, axis_index_groups=groups)  25.5 us
    pallas_call x1, Pallas kernels, grad_change(): pl.pallas_call(grad_body, grid=(hidden // block,), out_shape=(jax.ShapeDt...  14.7 us
    pallas_call x1, Pallas kernels, stencil_taps(): pl.pallas_call(taps_body, out_shape=jax.ShapeDtypeStruct((ROUNDS + 1, 8,...  13.9 us
    ppermute x5, waiting for transfers between devices, swap(): return lax.ppermute(value, 'grp', [(i, i ^ bit) for i in range(count)])  10.8 us
    ppermute x4, starting transfers between devices, shift(): lax.ppermute(value, axis, [(i, (i + step) % count) for i in range(count)])  7.98 us
    ppermute x5, starting transfers between devices, swap(): return lax.ppermute(value, 'grp', [(i, i ^ bit) for i in range(count)])  6.59 us
    pallas_call x1, Pallas kernels, stencil(): pl.pallas_call(stencil_body, grid=(lanes // block,), out_shape=jax.ShapeD...  3.9 us
    unnamed x15, local copies, waits for them, and re-layouts  3.3 us
  transfers between devices with their start and end apart: 11, of which 2 were waited for; matrix products, arithmetic and copies ran while one was open for 13% of the time, Pallas kernels for 30%

profile of v3, /device:TPU:5, one launch (start us, length us, event | category | flops | bytes accessed | tf_op | source)
XLA Modules:
  0.0 107.0 jit_solution(489082968291033214)
XLA Ops:
  0.6 1.9 %dynamic-slice_bitcast_fusion = bf16[192,1536]{1,0:T(8,128)(2,1)} fusion(bf16[1,1,384,1536]{3,2,1,0:T(8,128)(2,1)} %param.12, s32[]{:T(128)S(6)} %select_n.32), kind=kLoop, calls=%fused_computation.12 | loop fusion | bytes 1179652 | tf_op jit(solution)/shard_map/dynamic_slice | solution.py:237
  3.2 10.9 %all-to-all-start = ((bf16[16,24,1536]{2,1,0:T(8,128)(2,1)}), bf16[16,24,1536]{2,1,0:T(8,128)(2,1)S(1)}, u32[]{:S(2)}, u32[]{:S(2)}) async-start(bf16[16,24,1536]{2,1,0:T(8,128)(2,1)} %bitcast.18), calls=%async_computation | async-start | bytes 2359296 | tf_op jit(solution)/shard_map/all_to_all | solution.py:218
  14.1 1.7 %copy.11 = bf16[2048,384]{0,1:T(8,128)(2,1)S(1)} copy(bf16[2048,384]{1,0:T(8,128)(2,1)} %param.9) | data formatting | bytes 3145728 | tf_op args[0]
  15.9 2.2 %convert_add_fusion.1 = f32[192,1536]{1,0:T(8,128)} fusion(bf16[192,1536]{1,0:T(8,128)(2,1)S(1)} %collective-permute-done, bf16[1,1,384,1536]{3,2,1,0:T(8,128)(2,1)} %param.12, s32[]{:T(128)S(6)} %select_n.31), kind=kLoop, calls=%fused_computation.8 | loop fusion | flops 884736 | bytes 2359300 | tf_op jit(solution)/shard_map/add | solution.py:239
  18.1 1.1 %dynamic-slice_convert_fusion = bf16[96,1536]{1,0:T(8,128)(2,1)S(1)} fusion(f32[192,1536]{1,0:T(8,128)} %convert_add_fusion.1, s32[]{:T(128)S(6)} %select_n.35), kind=kLoop, calls=%fused_computation.11 | loop fusion | bytes 589828 | tf_op jit(solution)/shard_map/convert_element_type | solution.py:240
  19.2 1.0 collective-permute-start.1
  20.6 13.9 %stencil_taps.1.taps_ref = f32[5,8,128]{2,1,0:T(8,128)} custom-call(s32[1]{0:T(128)} %bitcast.7.lag_ref, s32[4]{0:T(128)} %num_ref.1, s32[4]{0:T(128)} %den_ref.1), custom_call_target="tpu_custom_call" | custom-call | tf_op jit(solution)/shard_map/stencil_taps/pallas_call | solution.py:166
  34.4 1.8 %fusion.4 = bf16[96,1536]{1,0:T(8,128)(2,1)} fusion(bf16[96,1536]{1,0:T(8,128)(2,1)S(1)} %collective-permute-done.1, f32[192,1536]{1,0:T(8,128)} %convert_add_fusion.1, s32[]{:T(128)S(6)} %select_n.34), kind=kLoop, calls=%fused_computation.13 | loop fusion | flops 442368 | bytes 1179652 | tf_op jit(solution)/shard_map/convert_element_type | solution.py:243
  36.3 1.2 %collective-permute-start.2 = (bf16[96,1536]{1,0:T(8,128)(2,1)}, bf16[96,1536]{1,0:T(8,128)(2,1)}, u32[]{:S(2)}, u32[]{:S(2)}) collective-permute-start(bf16[96,1536]{1,0:T(8,128)(2,1)} %fusion.4), channel_id=1, source_target_pairs={{0,4},{4,8},{8,12},{12,16},{16,20},{20,24},{24,28},{28,32},{32,36}... | collective-permute-start | bytes 884744 | tf_op jit(solution)/shard_map/ppermute | solution.py:131
  37.4 3.9 %collective-permute-start.3 = (bf16[96,1536]{1,0:T(8,128)(2,1)}, bf16[96,1536]{1,0:T(8,128)(2,1)}, u32[]{:S(2)}, u32[]{:S(2)}) collective-permute-start(bf16[96,1536]{1,0:T(8,128)(2,1)} %fusion.4), channel_id=1, source_target_pairs={{0,252},{4,0},{8,4},{12,8},{16,12},{20,16},{24,20},{28,24},{32,28}... | collective-permute-start | bytes 884744 | tf_op jit(solution)/shard_map/ppermute | solution.py:131
  41.4 1.4 %collective-permute-start.7 = (bf16[4,24,1536]{2,1,0:T(8,128)(2,1)S(1)}, bf16[4,24,1536]{2,1,0:T(8,128)(2,1)S(1)}, u32[]{:S(2)}, u32[]{:S(2)}) collective-permute-start(bf16[4,24,1536]{2,1,0:T(8,128)(2,1)S(1)} %get-tuple-element.13), channel_id=1, source_target_pairs={{0,64},{4,68},{8,72},{12,76},{16,80},{20,84},{24,88},{28,92},{32,9... | collective-permute-start | bytes 884744 | tf_op jit(solution)/shard_map/ppermute | solution.py:131
  42.8 1.5 %collective-permute-start.8 = (bf16[4,24,1536]{2,1,0:T(8,128)(2,1)S(1)}, bf16[4,24,1536]{2,1,0:T(8,128)(2,1)}, u32[]{:S(2)}, u32[]{:S(2)}) collective-permute-start(bf16[4,24,1536]{2,1,0:T(8,128)(2,1)S(1)} %get-tuple-element.12), channel_id=1, source_target_pairs={{0,192},{4,196},{8,200},{12,204},{16,208},{20,212},{24,216},{28,22... | collective-permute-start | bytes 884744 | tf_op jit(solution)/shard_map/ppermute | solution.py:131
  44.3 1.6 %fusion.6.turned_ref = bf16[384,2048]{1,0:T(8,128)(2,1)} fusion(f32[2048]{0:T(1024)S(1)} %add_rsqrt_fusion, bf16[2048,384]{0,1:T(8,128)(2,1)S(1)} %copy.11), kind=kLoop, calls=%fused_computation.17 | loop fusion | flops 2359296 | bytes 3153920 | tf_op jit(solution)/shard_map/transpose | solution.py:259
  45.9 2.8 %collective-permute-done.7.below_ref = bf16[4,24,1536]{2,1,0:T(8,128)(2,1)S(1)} collective-permute-done((bf16[4,24,1536]{2,1,0:T(8,128)(2,1)S(1)}, bf16[4,24,1536]{2,1,0:T(8,128)(2,1)S(1)}, u32[]{:S(2)}, u32[]{:S(2)}) %collective-permute-start.7) | collective-permute-done | bytes 294944 | tf_op jit(solution)/shard_map/ppermute | solution.py:131
  49.5 3.9 %stencil.1 = bf16[16,24,1536]{2,1,0:T(8,128)(2,1)} custom-call(f32[5,8,128]{2,1,0:T(8,128)} %stencil_taps.1.taps_ref, bf16[4,24,1536]{2,1,0:T(8,128)(2,1)} %copy-done.2, bf16[16,24,1536]{2,1,0:T(8,128)(2,1)} %copy-done, bf16[4,24,1536]{2,1,0:T(8,128)(2,1)} %collective-permute-done.8.above_ref), custom_call_target="tpu_custom_call" | custom-call | flops 8257536 | bytes 2359296 | tf_op jit(solution)/shard_map/stencil/pallas_call | solution.py:201
  53.4 14.6 %all-to-all-start.1 = ((bf16[16,24,1536]{2,1,0:T(8,128)(2,1)}), bf16[16,24,1536]{2,1,0:T(8,128)(2,1)}, u32[]{:S(2)}, u32[]{:S(2)}) async-start(bf16[16,24,1536]{2,1,0:T(8,128)(2,1)} %stencil.1), calls=%async_computation.1 | async-start | bytes 2359296 | tf_op jit(solution)/shard_map/all_to_all | solution.py:218
  68.0 1.4 %multiply_convert_fusion.first_ref = bf16[96,1536]{1,0:T(8,128)(2,1)S(1)} fusion(bf16[96,1536]{1,0:T(8,128)(2,1)} %collective-permute-done.3, bf16[96,1536]{1,0:T(8,128)(2,1)} %collective-permute-done.2, bf16[96,1536]{1,0:T(8,128)(2,1)S(1)} %collective-permute-done.1, f32[192,1536]{1,0:T(8,128)} %convert_add_fusion.1, s32[]{:T(128)S(6)} %select_n.34), kind=kLoop, calls=%fused_computation.9 | loop fusion | flops 1179648 | bytes 1769476 | tf_op jit(solution)/shard_map/convert_element_type | solution.py:245
  70.8 2.0 %collective-permute-start.5 = (bf16[96,1536]{1,0:T(8,128)(2,1)S(1)}, bf16[96,1536]{1,0:T(8,128)(2,1)S(1)}, u32[]{:S(2)}, u32[]{:S(2)}) collective-permute-start(bf16[96,1536]{1,0:T(8,128)(2,1)S(1)} %multiply_convert_fusion.first_ref), channel_id=1, source_target_pairs={{0,1},{1,0},{2,3},{3,2},{4,5},{5,4},{6,7},{7,6},{8,9},{9,8},{10,11... | collective-permute-start | bytes 884744 | tf_op jit(solution)/shard_map/ppermute | solution.py:136
  72.8 10.8 %collective-permute-done.4.second_ref = bf16[96,1536]{1,0:T(8,128)(2,1)} collective-permute-done((bf16[96,1536]{1,0:T(8,128)(2,1)S(1)}, bf16[96,1536]{1,0:T(8,128)(2,1)}, u32[]{:S(2)}, u32[]{:S(2)}) %collective-permute-start.4) | collective-permute-done | bytes 294944 | tf_op jit(solution)/shard_map/ppermute | solution.py:136
  83.6 1.9 %collective-permute-start.6 = (bf16[96,1536]{1,0:T(8,128)(2,1)}, bf16[96,1536]{1,0:T(8,128)(2,1)S(1)}, u32[]{:S(2)}, u32[]{:S(2)}) collective-permute-start(bf16[96,1536]{1,0:T(8,128)(2,1)} %collective-permute-done.4.second_ref), channel_id=1, source_target_pairs={{0,1},{1,0},{2,3},{3,2},{4,5},{5,4},{6,7},{7,6},{8,9},{9,8},{10,11... | collective-permute-start | bytes 884744 | tf_op jit(solution)/shard_map/ppermute | solution.py:136
  85.6 1.4 %broadcast_select_fusion.masked_ref = bf16[2048,384]{1,0:T(8,128)(2,1)} fusion(bf16[2048,384]{1,0:T(8,128)(2,1)S(1)} %copy-done.1, pred[2048]{0:T(1024)(128)(4,1)S(1)} %broadcast_compare_fusion), kind=kLoop, calls=%fused_computation.6 | loop fusion | flops 786432 | bytes 3147776 | tf_op jit(solution)/shard_map/jit(_where)/select_n | solution.py:258
  86.9 1.6 %copy.12.normed_ref = bf16[2048,384]{1,0:T(8,128)(2,1)} copy(bf16[2048,384]{0,1:T(8,128)(2,1)S(1)} %fusion.1) | data formatting | bytes 3145728 | tf_op jit(solution)/shard_map/optimization_barrier | solution.py:259
  89.4 14.7 %grad_change.1 = (bf16[384,1536]{1,0:T(8,128)(2,1)}, bf16[384,1536]{1,0:T(8,128)(2,1)}) custom-call(s32[1]{0:T(128)} %bitcast.member_ref, bf16[2048,384]{1,0:T(8,128)(2,1)} %copy.12.normed_ref, bf16[384,2048]{1,0:T(8,128)(2,1)} %fusion.6.turned_ref, bf16[2048,384]{1,0:T(8,128)(2,1)} %broadcast_select_fusion.masked_ref, bf16[96,1536]{1,0:T(8,128)(2,1)} %copy-done.3, ...), custom_call_target="tpu_custom_call" | custom-call | flops 7247757312 | bytes 8257536 | tf_op jit(solution)/shard_map/grad_change/pallas_call | solution.py:92
  104.1 2.9 %fusion.3 = bf16[1,1,384,1536]{3,2,1,0:T(8,128)(2,1)} fusion(bf16[384,1536]{1,0:T(8,128)(2,1)} %get-tuple-element.11, bf16[16,24,1536]{2,1,0:T(8,128)(2,1)} %all-to-all-done.1), kind=kLoop, calls=%fused_computation.7 | loop fusion | flops 2359296 | bytes 3538944 | tf_op jit(solution)/shard_map/broadcast_in_dim | solution.py:264
  (30 shorter events, 4.1 us)
Async XLA Ops:
  2.6 13.3 %collective-permute-start = (bf16[192,1536]{1,0:T(8,128)(2,1)}, bf16[192,1536]{1,0:T(8,128)(2,1)S(1)}, u32[]{:S(2)}, u32[]{:S(2)}) collective-permute-start(bf16[192,1536]{1,0:T(8,128)(2,1)} %dynamic-slice_bitcast_fusion), channel_id=1, source_target_pairs={{0,1},{1,0},{2,3},{3,2},{4,5},{5,4},{6,7},{7,6},{8,9},{9,8},{10,11... | collective-permute-start | bytes 1769480 | tf_op jit(solution)/shard_map/ppermute | solution.py:136
  3.2 38.1 %all-to-all-start = ((bf16[16,24,1536]{2,1,0:T(8,128)(2,1)}), bf16[16,24,1536]{2,1,0:T(8,128)(2,1)S(1)}, u32[]{:S(2)}, u32[]{:S(2)}) async-start(bf16[16,24,1536]{2,1,0:T(8,128)(2,1)} %bitcast.18), calls=%async_computation | async-start | bytes 2359296 | tf_op jit(solution)/shard_map/all_to_all | solution.py:218
  19.2 15.2 %collective-permute-start.1 = (bf16[96,1536]{1,0:T(8,128)(2,1)S(1)}, bf16[96,1536]{1,0:T(8,128)(2,1)S(1)}, u32[]{:S(2)}, u32[]{:S(2)}) collective-permute-start(bf16[96,1536]{1,0:T(8,128)(2,1)S(1)} %dynamic-slice_convert_fusion), channel_id=1, source_target_pairs={{0,2},{1,3},{2,0},{3,1},{4,6},{5,7},{6,4},{7,5},{8,10},{9,11},{10,... | collective-permute-start | bytes 884744 | tf_op jit(solution)/shard_map/ppermute | solution.py:136
  36.3 31.7 %collective-permute-start.2 = (bf16[96,1536]{1,0:T(8,128)(2,1)}, bf16[96,1536]{1,0:T(8,128)(2,1)}, u32[]{:S(2)}, u32[]{:S(2)}) collective-permute-start(bf16[96,1536]{1,0:T(8,128)(2,1)} %fusion.4), channel_id=1, source_target_pairs={{0,4},{4,8},{8,12},{12,16},{16,20},{20,24},{24,28},{28,32},{32,36}... | collective-permute-start | bytes 884744 | tf_op jit(solution)/shard_map/ppermute | solution.py:131
  37.4 30.5 %collective-permute-start.3 = (bf16[96,1536]{1,0:T(8,128)(2,1)}, bf16[96,1536]{1,0:T(8,128)(2,1)}, u32[]{:S(2)}, u32[]{:S(2)}) collective-permute-start(bf16[96,1536]{1,0:T(8,128)(2,1)} %fusion.4), channel_id=1, source_target_pairs={{0,252},{4,0},{8,4},{12,8},{16,12},{20,16},{24,20},{28,24},{32,28}... | collective-permute-start | bytes 884744 | tf_op jit(solution)/shard_map/ppermute | solution.py:131
  41.3 4.5 %copy-start = (bf16[16,24,1536]{2,1,0:T(8,128)(2,1)}, bf16[16,24,1536]{2,1,0:T(8,128)(2,1)S(1)}, u32[]{:S(2)}) copy-start(bf16[16,24,1536]{2,1,0:T(8,128)(2,1)S(1)} %all-to-all-done.cells_ref) | copy-start | bytes 3538948
  41.4 7.3 %collective-permute-start.7 = (bf16[4,24,1536]{2,1,0:T(8,128)(2,1)S(1)}, bf16[4,24,1536]{2,1,0:T(8,128)(2,1)S(1)}, u32[]{:S(2)}, u32[]{:S(2)}) collective-permute-start(bf16[4,24,1536]{2,1,0:T(8,128)(2,1)S(1)} %get-tuple-element.13), channel_id=1, source_target_pairs={{0,64},{4,68},{8,72},{12,76},{16,80},{20,84},{24,88},{28,92},{32,9... | collective-permute-start | bytes 884744 | tf_op jit(solution)/shard_map/ppermute | solution.py:131
  42.8 6.0 %collective-permute-start.8 = (bf16[4,24,1536]{2,1,0:T(8,128)(2,1)S(1)}, bf16[4,24,1536]{2,1,0:T(8,128)(2,1)}, u32[]{:S(2)}, u32[]{:S(2)}) collective-permute-start(bf16[4,24,1536]{2,1,0:T(8,128)(2,1)S(1)} %get-tuple-element.12), channel_id=1, source_target_pairs={{0,192},{4,196},{8,200},{12,204},{16,208},{20,212},{24,216},{28,22... | collective-permute-start | bytes 884744 | tf_op jit(solution)/shard_map/ppermute | solution.py:131
  48.7 0.7 copy-start.2
  53.4 50.7 %all-to-all-start.1 = ((bf16[16,24,1536]{2,1,0:T(8,128)(2,1)}), bf16[16,24,1536]{2,1,0:T(8,128)(2,1)}, u32[]{:S(2)}, u32[]{:S(2)}) async-start(bf16[16,24,1536]{2,1,0:T(8,128)(2,1)} %stencil.1), calls=%async_computation.1 | async-start | bytes 2359296 | tf_op jit(solution)/shard_map/all_to_all | solution.py:218
  69.4 1.5 %copy-start.3 = (bf16[96,1536]{1,0:T(8,128)(2,1)}, bf16[96,1536]{1,0:T(8,128)(2,1)S(1)}, u32[]{:S(2)}) copy-start(bf16[96,1536]{1,0:T(8,128)(2,1)S(1)} %multiply_convert_fusion.first_ref) | copy-start | bytes 884740
  69.4 1.4 %copy-start.4 = (s32[2048]{0:T(1024)S(1)}, s32[2048]{0:T(1024)}, u32[]{:S(2)}) copy-start(s32[2048]{0:T(1024)} %param.11) | copy-start | bytes 24580
  69.4 16.2 %copy-start.1 = (bf16[2048,384]{1,0:T(8,128)(2,1)S(1)}, bf16[2048,384]{1,0:T(8,128)(2,1)}, u32[]{:S(2)}) copy-start(bf16[2048,384]{1,0:T(8,128)(2,1)} %param.10) | copy-start | bytes 4718596
  69.4 14.2 %collective-permute-start.4 = (bf16[96,1536]{1,0:T(8,128)(2,1)S(1)}, bf16[96,1536]{1,0:T(8,128)(2,1)}, u32[]{:S(2)}, u32[]{:S(2)}) collective-permute-start(bf16[96,1536]{1,0:T(8,128)(2,1)S(1)} %multiply_convert_fusion.first_ref), channel_id=1, source_target_pairs={{0,2},{1,3},{2,0},{3,1},{4,6},{5,7},{6,4},{7,5},{8,10},{9,11},{10,... | collective-permute-start | bytes 884744 | tf_op jit(solution)/shard_map/ppermute | solution.py:136
  70.8 17.7 %collective-permute-start.5 = (bf16[96,1536]{1,0:T(8,128)(2,1)S(1)}, bf16[96,1536]{1,0:T(8,128)(2,1)S(1)}, u32[]{:S(2)}, u32[]{:S(2)}) collective-permute-start(bf16[96,1536]{1,0:T(8,128)(2,1)S(1)} %multiply_convert_fusion.first_ref), channel_id=1, source_target_pairs={{0,1},{1,0},{2,3},{3,2},{4,5},{5,4},{6,7},{7,6},{8,9},{9,8},{10,11... | collective-permute-start | bytes 884744 | tf_op jit(solution)/shard_map/ppermute | solution.py:136
  83.6 4.9 %collective-permute-start.6 = (bf16[96,1536]{1,0:T(8,128)(2,1)}, bf16[96,1536]{1,0:T(8,128)(2,1)S(1)}, u32[]{:S(2)}, u32[]{:S(2)}) collective-permute-start(bf16[96,1536]{1,0:T(8,128)(2,1)} %collective-permute-done.4.second_ref), channel_id=1, source_target_pairs={{0,1},{1,0},{2,3},{3,2},{4,5},{5,4},{6,7},{7,6},{8,9},{9,8},{10,11... | collective-permute-start | bytes 884744 | tf_op jit(solution)/shard_map/ppermute | solution.py:136
  88.5 0.7 copy-start.5
  88.5 0.9 copy-start.6
